TPU v7x, 32 devices: a whole 2x2x4 slice. The times are simulated.
32 devices in a mesh: ty: 16 (over z, y, core), tx: 2 (over x).
Axes of the slice: x: 2, y: 2, z: 4, core: 2. Of those that a mesh axis runs over, the one named last changes fastest.
Arguments:
- ctrl: float32 [16, 2, 512, 640], P('ty', 'tx'), may hold values from -6 to 6
- interp_wt: float32 [16, 2, 4, 128, 384], P('ty', 'tx'), may hold values from -0.3125 to 0.3125
- interp_cols: int32 [16, 2, 4, 384], P('ty', 'tx'), may hold values from 0 to 1023
- conv_wt: float32 [16, 2, 4, 128, 512], P('ty', 'tx'), may hold values from -0.25 to 0.25
- conv_cols: int32 [16, 2, 4, 512], P('ty', 'tx'), may hold values from 0 to 1023
- halo_index: int32 [16, 2, 8, 64], P('ty', 'tx'), may hold values from 0 to 511
- valid: int32 [16, 2], P('ty', 'tx'), may hold values from 256 to 512
Outputs:
- localized: float32 [16, 2, 512, 640], P('ty', 'tx')
Inputs may be any that keep to these rules, and one draw needn't show every extreme that they name: `interp_cols`: indices into a tile's extended subgrid of 1024 rows; repeats are allowed. `conv_cols`: indices into a tile's extended subgrid; repeats are allowed. `halo_index`: owned row indices; repeats are allowed.
All inputs are finite; a program needn't handle non-finite values.
Results may differ from a plain program's by a relative error of at most 0.0001.
Values sent between devices are 32-bit elements; how exact they have to be, the bound alone decides.
A program may use at most 64 MiB of HBM per device.

v0:
```python
import functools

import jax
import jax.numpy as jnp
from jax import lax
from jax.experimental import pallas as pl
from jax.experimental.pallas import tpu as pltpu
from jax.sharding import PartitionSpec as P

MESH = pl.DeviceIdType.MESH
DIRECTIONS = ((-1, -1), (-1, 0), (-1, 1), (0, -1), (0, 1), (1, -1), (1, 0), (1, 1))
ORDER = (0, 2, 5, 7, 3, 4, 1, 6)
F32, BF16 = jnp.float32, jnp.bfloat16


def halves(x):
    hi = x.astype(BF16)
    return hi, (x - hi.astype(F32)).astype(BF16)


def dot(a, b):
    return jnp.dot(a, b, preferred_element_type=F32)


def dot_nt(a, b):
    return lax.dot_general(a, b, (((1,), (1,)), ((), ())), preferred_element_type=F32)


def kernel(
    n_ty, n_tx, chunks, valid_ref, ctrl_hbm, iwt_hbm, icols_ref, cwt_hbm, ccols_ref, halo_ref,
    out_ref, iwt_ref, cwt_ref, imat, imat_t, cmat, cmat_t, pick, pick_t, *rest,
):
    n_chunks = len(chunks)
    send_sem, recv_sem, load_sem, store_sem = rest[-4:]
    buffers = rest[:-4]
    own = buffers[:n_chunks]
    rhs = buffers[n_chunks : 2 * n_chunks]
    send = [buffers[(2 + e) * n_chunks : (3 + e) * n_chunks] for e in range(4)]
    recv = [buffers[(6 + e) * n_chunks : (7 + e) * n_chunks] for e in range(4)]
    loads = [pltpu.make_async_copy(iwt_hbm, iwt_ref, load_sem.at[0])]
    for c, (lo, width) in enumerate(chunks):
        loads.append(
            pltpu.make_async_copy(ctrl_hbm.at[:, lo : lo + width], own[c], load_sem.at[1 + c])
        )
    loads.append(pltpu.make_async_copy(cwt_hbm, cwt_ref, load_sem.at[1 + n_chunks]))
    for item in loads:
        item.start()
    ty, tx = lax.axis_index("ty"), lax.axis_index("tx")
    rows = out_ref.shape[0]
    n_own = own[0].shape[0]
    n_slot = recv[0][0].shape[0]
    slot = n_slot // 8
    extent = n_own + n_slot

    def there(off):
        return jnp.logical_and(ty + off >= 0, ty + off < n_ty)

    def peer(row_off, col_off):
        return ty + row_off, lax.rem(tx + col_off + n_tx, n_tx)

    barrier = pltpu.get_barrier_semaphore()
    for row_off, col_off in DIRECTIONS:
        @pl.when(there(row_off))
        def _():
            pl.semaphore_signal(
                barrier, inc=1, device_id=peer(row_off, col_off), device_id_type=MESH
            )

    def copy(e, c, d):
        sign = -1 if e < 2 else 1
        row_off, col_off = DIRECTIONS[d]
        piece = pl.ds(d * slot, slot)
        return pltpu.make_async_remote_copy(
            src_ref=send[e][c].at[piece],
            dst_ref=recv[e][c].at[piece],
            send_sem=send_sem.at[e, c, d],
            recv_sem=recv_sem.at[e, c, d],
            device_id=peer(sign * row_off, sign * col_off),
            device_id_type=MESH,
        )

    def each(e, c, sending, action):
        sign = -1 if e < 2 else 1
        for d in ORDER:
            row_off = DIRECTIONS[d][0] * (sign if sending else -sign)
            if row_off == 0:
                action(copy(e, c, d))
            else:
                pl.when(there(row_off))(functools.partial(lambda e, c, d: action(copy(e, c, d)), e, c, d))

    def start(e, c):
        each(e, c, True, lambda item: item.start())

    def arrived(e, c):
        each(e, c, False, lambda item: item.wait_recv())

    def spread(wt_ref, cols_ref, mat, mat_t, base=0, count=extent):
        blocks, height, width = wt_ref.shape
        for b in range(blocks):
            index = cols_ref[b : b + 1, :]
            place_of = lax.broadcasted_iota(jnp.int32, (count, width), 0) + base
            hot = (place_of == index).astype(F32).astype(BF16)
            hi, lo = halves(wt_ref[b])
            span = pl.ds(b * height, height)
            if mat is not None:
                mat[0, span], mat[1, span] = halves(dot_nt(hi, hot) + dot_nt(lo, hot))
            if mat_t is not None:
                part = pl.ds(base, count)
                mat_t[0, part, span], mat_t[1, part, span] = halves(dot_nt(hot, hi) + dot_nt(hot, lo))

    def product(mat, row0, count, col0, depth, c, base):
        a_hi = mat[0, row0 : row0 + count, col0 : col0 + depth]
        a_lo = mat[1, row0 : row0 + count, col0 : col0 + depth]
        b_hi, b_lo = rhs[c][0, base : base + depth], rhs[c][1, base : base + depth]
        return dot(a_hi, b_hi) + (dot(a_hi, b_lo) + dot(a_lo, b_hi))

    def gathered(e, c):
        hi, lo = halves(recv[e][c][...])
        return dot(pick_t[...], hi) + dot(pick_t[...], lo)

    def place(c, base, value):
        rhs[c][0, base : base + value.shape[0]], rhs[c][1, base : base + value.shape[0]] = halves(value)

    def picked(c):
        return dot(pick[...], rhs[c][0, :n_own]) + dot(pick[...], rhs[c][1, :n_own])

    for e in range(4):
        sign = -1 if e < 2 else 1
        for d, (row_off, _) in enumerate(DIRECTIONS):
            if row_off:
                @pl.when(jnp.logical_not(there(-sign * row_off)))
                def _():
                    for c in range(n_chunks):
                        piece = recv[e][c].at[pl.ds(d * slot, slot)]
                        piece[...] = jnp.zeros(piece.shape, F32)

    loads[0].wait()
    spread(iwt_ref, icols_ref, None, imat_t, n_own, n_slot)
    limit = valid_ref[0, 0]
    edge = jnp.int32(2)
    edge += jnp.where(there(-1), 3, 0) + jnp.where(there(1), 3, 0)
    pl.semaphore_wait(barrier, edge)

    def keep(width):
        return lax.broadcasted_iota(jnp.int32, (rows, width), 0) < limit

    for c, (lo, width) in enumerate(chunks):
        loads[1 + c].wait()
        place(c, 0, jnp.where(keep(width), own[c][...], 0.0))
        send[0][c][...] = product(imat_t, n_own, n_slot, 0, rows, c, 0)
        start(0, c)
    spread(iwt_ref, icols_ref, None, imat_t, 0, n_own)
    for c in range(n_chunks):
        own[c][...] = product(imat_t, 0, n_own, 0, rows, c, 0)
    halo = jnp.concatenate([halo_ref[d : d + 1, :] for d in range(8)], axis=1)
    hot = (lax.broadcasted_iota(jnp.int32, (n_own, n_slot), 0) == halo).astype(F32)
    loads[-1].wait()
    pick_t[...] = hot.astype(BF16)
    pick[...] = hot.T.astype(BF16)
    spread(cwt_ref, ccols_ref, None, cmat_t)
    for c in range(n_chunks):
        arrived(0, c)
        place(c, 0, own[c][...] + gathered(0, c))
        send[1][c][...] = product(cmat_t, n_own, n_slot, 0, n_own, c, 0)
        start(1, c)
        own[c][...] = product(cmat_t, 0, n_own, 0, n_own, c, 0)
    spread(cwt_ref, ccols_ref, cmat, None)
    spread(iwt_ref, icols_ref, imat, None)
    for c in range(n_chunks):
        arrived(1, c)
        place(c, 0, own[c][...] + gathered(1, c))
        send[2][c][...] = picked(c)
        start(2, c)
        own[c][...] = product(cmat, 0, n_own, 0, n_own, c, 0)
    for c in range(n_chunks):
        arrived(2, c)
        place(c, n_own, recv[2][c][...])
        place(c, 0, own[c][...] + product(cmat, 0, n_own, n_own, n_slot, c, n_own))
        send[3][c][...] = picked(c)
        start(3, c)
        own[c][...] = product(imat, 0, rows, 0, n_own, c, 0)
    stores = []
    for c, (lo, width) in enumerate(chunks):
        arrived(3, c)
        place(c, n_own, recv[3][c][...])
        total = own[c][...] + product(imat, 0, rows, n_own, n_slot, c, n_own)
        own[c][...] = jnp.where(keep(width), total, 0.0)
        stores.append(
            pltpu.make_async_copy(own[c], out_ref.at[:, lo : lo + width], store_sem.at[c])
        )
        stores[c].start()
    for e in range(4):
        for c in range(n_chunks):
            each(e, c, True, lambda item: item.wait_send())
    for item in stores:
        item.wait()


def solution(mesh):
    n_ty, n_tx = mesh.shape["ty"], mesh.shape["tx"]

    def body(ctrl, interp_wt, interp_cols, conv_wt, conv_cols, halo_index, valid):
        rows, feat = ctrl.shape[2:]
        n_own = conv_wt.shape[2] * conv_wt.shape[3]
        n_slot = halo_index.shape[2] * halo_index.shape[3]
        extent = n_own + n_slot
        tiles = feat // 128
        first = 128 * max(tiles - tiles // 2, 1)
        chunks = ((0, first), (first, feat - first)) if feat > first else ((0, feat),)
        widths = [width for _, width in chunks]
        pin = functools.partial(pltpu.with_memory_space_constraint, memory_space=pltpu.HBM)
        hbm = pl.BlockSpec(memory_space=pltpu.HBM)
        vmem = pl.BlockSpec(memory_space=pltpu.VMEM)
        scratch = [
            pltpu.VMEM(interp_wt.shape[2:], F32),
            pltpu.VMEM(conv_wt.shape[2:], F32),
            pltpu.VMEM((2, rows, extent), BF16),
            pltpu.VMEM((2, extent, rows), BF16),
            pltpu.VMEM((2, n_own, extent), BF16),
            pltpu.VMEM((2, extent, n_own), BF16),
            pltpu.VMEM((n_slot, n_own), BF16),
            pltpu.VMEM((n_own, n_slot), BF16),
        ]
        assert rows == n_own
        scratch += [pltpu.VMEM((n_own, width), F32) for width in widths]
        scratch += [pltpu.VMEM((2, extent, width), BF16) for width in widths]
        scratch += [pltpu.VMEM((n_slot, width), F32) for _ in range(8) for width in widths]
        scratch += [pltpu.SemaphoreType.DMA((4, len(chunks), 8))] * 2
        scratch += [pltpu.SemaphoreType.DMA((2 + len(chunks),)), pltpu.SemaphoreType.DMA((len(chunks),))]
        out = pl.pallas_call(
            functools.partial(kernel, n_ty, n_tx, chunks),
            out_shape=jax.ShapeDtypeStruct((rows, feat), F32),
            in_specs=[pl.BlockSpec(memory_space=pltpu.SMEM), hbm, hbm, vmem, hbm, vmem, vmem],
            out_specs=pl.BlockSpec(memory_space=pl.ANY),
            scratch_shapes=scratch,
            compiler_params=pltpu.CompilerParams(
                collective_id=0, has_side_effects=True, vmem_limit_bytes=44 * 1024 * 1024
            ),
        )(
            valid, pin(ctrl[0, 0]), pin(interp_wt[0, 0]), pin(interp_cols[0, 0]), pin(conv_wt[0, 0]),
            pin(conv_cols[0, 0]), pin(halo_index[0, 0]),
        )
        return out[None, None]

    placed = (
        P("ty", "tx", None, None),
        P("ty", "tx", None, None, None),
        P("ty", "tx", None, None),
        P("ty", "tx", None, None, None),
        P("ty", "tx", None, None),
        P("ty", "tx", None, None),
        P("ty", "tx"),
    )
    return jax.shard_map(
        body, mesh=mesh, in_specs=placed, out_specs=P("ty", "tx", None, None), check_vma=False
    )
```

profile of v0, /device:TPU:17, one launch (start us, length us, event | category | flops | bytes accessed | tf_op | source)
XLA Modules:
  0.0 95.1 jit_solution(2358142841932632508)
XLA Ops:
  0.7 93.4 %shard_map.73 = f32[512,640]{1,0:T(8,128)S(1)} custom-call(s32[1,1]{1,0:T(1,128)S(6)} %copy.9.valid_ref, f32[512,640]{1,0:T(8,128)} %bitcast.8, f32[4,128,384]{2,1,0:T(8,128)} %bitcast.10, s32[4,384]{1,0:T(4,128)} %bitcast.12, f32[4,128,512]{2,1,0:T(8,128)} %bitcast.9, s32[4,512]{1,0:T(4,128)} %bitcast.11, s32[8,64]{1,0:T(8,128)} %bitcast.13), custom_call_target="tpu_custom_call" | custom-call | tf_op jit(solution)/shard_map/pallas_call | solution.py:230
  94.1 1.1 %copy.10 = f32[1,1,512,640]{3,2,1,0:T(8,128)} copy(f32[1,1,512,640]{3,2,1,0:T(8,128)S(1)} %bitcast.7) | data formatting | bytes 2621440
where the time goes:
time: 96.2 us; the launch traced here: 95.1 us
  Pallas kernels  93.4 us (97%)
  local copies, waits for them, and re-layouts  1.06 us (1%)
    pallas_call x1, Pallas kernels, body(): pl.pallas_call(functools.partial(kernel, n_ty, n_tx, chunks), out_shape=j...  93.4 us

commit v1 on v0

--- a/solution.py
+++ b/solution.py
@@ -195,6 +195,385 @@
     for item in stores:
         item.wait()
 
+OWN_ORDER = (0, 2, 3, 4, 5, 7, 1, 6)
+FAR_ORDER = (0, 2, 3, 4, 5, 7, 6, 1)
+
+
+def stacked(x):
+    hi, lo = halves(x)
+    return hi, jnp.concatenate([hi, lo], axis=0)
+
+
+def folded(x):
+    half = x.shape[0] // 2
+    return x[:half] + x[half:]
+
+
+def pair_kernel(
+    n_ty, cuts, valid_ref, ctrl_hbm, iwt_hbm, icols_ref, cwt_hbm, ccols_ref, halo_ref,
+    out_ref, ctrl, iwt, cwt, cwt_f, ccols_f, halo_f, xt, imat, cmat, pick,
+    zp, aslot, r1a, zf, r1o, r1f, bown, s2, r2, loc2, s3, r3, loc3, vacc,
+    s4o, s4f, loc4, v_r, r4x, r4y, s5, r5, out_t, send_sem, recv_sem, load_sem,
+):
+    rows, feat = ctrl.shape
+    half = feat // 2
+    n_own, n_slot = pick.shape[1:]
+    slot, group = n_slot // 8, n_slot // 4
+    extent = n_own + n_slot
+    n_x = 3 * group
+    blocks = cwt.shape[0]
+    ty, tx = lax.axis_index("ty"), lax.axis_index("tx")
+    far = 1 - tx
+
+    loads = [
+        pltpu.make_async_copy(cwt_hbm, cwt, load_sem.at[0]),
+        pltpu.make_async_copy(iwt_hbm, iwt, load_sem.at[1]),
+        pltpu.make_async_copy(ctrl_hbm, ctrl, load_sem.at[2]),
+    ]
+    for item in loads:
+        item.start()
+
+    def there(off):
+        return jnp.logical_and(ty + off >= 0, ty + off < n_ty)
+
+    barrier = pltpu.get_barrier_semaphore()
+    partners = [(0, 1), (-1, 0), (1, 0), (-1, 1), (1, 1)]
+    for row_off, flip in partners:
+        def greet(row_off=row_off, flip=flip):
+            pl.semaphore_signal(
+                barrier, inc=1, device_id=(ty + row_off, far if flip else tx), device_id_type=MESH
+            )
+        if row_off:
+            pl.when(there(row_off))(greet)
+        else:
+            greet()
+
+    flows = []
+
+    class Flow:
+        def __init__(self, src, dst, row_off, flip):
+            self.row_off = row_off
+            self.key = len(flows)
+            flows.append(self)
+            self.copy = pltpu.make_async_remote_copy(
+                src_ref=src, dst_ref=dst, send_sem=send_sem.at[self.key], recv_sem=recv_sem.at[self.key],
+                device_id=(ty + row_off, far if flip else tx), device_id_type=MESH,
+            )
+
+        def act(self, sign, action):
+            if self.row_off:
+                pl.when(there(sign * self.row_off))(action)
+            else:
+                action()
+
+        def start(self):
+            self.act(1, lambda: self.copy.start())
+
+        def arrived(self):
+            self.act(-1, lambda: self.copy.wait_recv())
+
+        def sent(self):
+            self.act(1, lambda: self.copy.wait_send())
+
+    def go(*items):
+        for item in items:
+            item.start()
+        return list(items)
+
+    def wait(items):
+        for item in items:
+            item.arrived()
+
+    def lane(count, width=group):
+        return lax.broadcasted_iota(jnp.int32, (count, width), 1)
+
+    def blend(first, second):
+        return jnp.where(lane(first.shape[0]) < slot, first, second)
+
+    def dense(mat, b, weights, index, order):
+        where = index
+        for place, d in enumerate(order):
+            low = n_own + d * slot
+            inside = jnp.logical_and(index >= low, index < low + slot)
+            where = jnp.where(inside, index + (place - d) * slot, where)
+        height, width = weights.shape
+        hot = lax.broadcasted_iota(jnp.int32, (extent, width), 0) == where
+        _, both = stacked(weights)
+        span = pl.ds(b * height, height)
+        mat[0, span], mat[1, span] = halves(folded(dot_nt(both, hot.astype(F32).astype(BF16))))
+
+    def choose(t, ref, order):
+        halo = jnp.concatenate([ref[d : d + 1, :] for d in order], axis=1)
+        hot = lax.broadcasted_iota(jnp.int32, (n_own, n_slot), 0) == halo
+        pick[t] = hot.astype(F32).astype(BF16)
+
+    def scatter(t, pieces, lo=0):
+        _, both = stacked(jnp.concatenate(pieces, axis=1) if len(pieces) > 1 else pieces[0])
+        return folded(dot_nt(both, pick[t, :, lo : lo + group * len(pieces)]))
+
+    def apply(x, mat, lo, count):
+        hi, both = x
+        return folded(dot(both, mat[0, :, lo : lo + count])) + dot(hi, mat[1, :, lo : lo + count])
+
+    def apply_nt(x, mat, lo, count):
+        hi, both = x
+        return folded(dot_nt(both, mat[0, :, lo : lo + count])) + dot_nt(hi, mat[1, :, lo : lo + count])
+
+    def gather(t, both, lo, count):
+        return folded(dot(both, pick[t, :, lo : lo + count]))
+
+    def mine(lo, count):
+        return pl.ds(pl.multiple_of(tx * half + lo, 16), count)
+
+    def theirs(lo, count):
+        return pl.ds(pl.multiple_of(far * half + lo, 16), count)
+
+    def blank(ref):
+        ref[...] = jnp.zeros(ref.shape, ref.dtype)
+
+    @pl.when(jnp.logical_not(there(-1)))
+    def _():
+        for ref in (
+            r1a.at[0], r1o.at[0], r1f.at[0], r2.at[0], r2.at[1], r2.at[2],
+            r3.at[3], r3.at[4], r3.at[5], r4x.at[2], r4y.at[1], r5.at[1],
+        ):
+            blank(ref)
+
+    @pl.when(jnp.logical_not(there(1)))
+    def _():
+        for ref in (
+            r1a.at[1], r1o.at[2], r1f.at[1], r2.at[3], r2.at[4], r2.at[5],
+            r3.at[0], r3.at[1], r3.at[2], r4x.at[0], r4y.at[0], r5.at[0],
+        ):
+            blank(ref)
+
+    loads[0].wait()
+    pl.semaphore_wait(barrier, 1 + jnp.where(there(-1), 2, 0) + jnp.where(there(1), 2, 0))
+    tables = go(Flow(ccols_ref, ccols_f, 0, 1), Flow(halo_ref, halo_f, 0, 1))
+    weights = go(*[Flow(cwt.at[b], cwt_f.at[b], 0, 1) for b in range(blocks)])
+
+    limit = valid_ref[0, 0]
+    loads[1].wait()
+    for b in range(iwt.shape[0]):
+        dense(imat, b, iwt[b], icols_ref[b : b + 1, :], OWN_ORDER)
+    loads[2].wait()
+    tile = 128
+    for lo in range(0, feat, tile):
+        live = lax.broadcasted_iota(jnp.int32, (rows, tile), 0) < limit
+        piece = jnp.where(live, ctrl[:, lo : lo + tile], 0.0).T
+        xt[0, lo : lo + tile], xt[1, lo : lo + tile] = halves(piece)
+    for lo in (0, half):
+        hi = xt[0, lo : lo + half]
+        both = jnp.concatenate([hi, xt[1, lo : lo + half]], axis=0)
+        value = apply((hi, both), imat, n_own, n_slot)
+        for g in range(4):
+            aslot[g, lo : lo + half] = value[:, g * group : (g + 1) * group]
+    first = go(Flow(aslot.at[3], r1a.at[0], 1, 0), Flow(aslot.at[3], r1a.at[1], -1, 0))
+    for lo in (0, half):
+        hi = xt[0, lo : lo + half]
+        both = jnp.concatenate([hi, xt[1, lo : lo + half]], axis=0)
+        zp[lo : lo + half] = apply((hi, both), imat, 0, n_own)
+    choose(0, halo_ref, OWN_ORDER)
+    wait(first)
+    for lo in (0, half):
+        span = slice(lo, lo + half)
+        zp[span] = zp[span] + scatter(0, [blend(r1a[0, span], r1a[1, span])], n_x)
+    crossed = []
+    for lo, count in cuts:
+        span = pl.ds(lo, count)
+        away, here = theirs(lo, count), mine(lo, count)
+        crossed.append(go(
+            Flow(zp.at[away], zf.at[span], 0, 1),
+            Flow(aslot.at[1, away], r1o.at[1, span], 0, 1),
+            Flow(aslot.at[0, away], r1o.at[0, span], 1, 1),
+            Flow(aslot.at[2, away], r1o.at[2, span], -1, 1),
+            Flow(aslot.at[0, here], r1f.at[0, span], 1, 0),
+            Flow(aslot.at[2, here], r1f.at[1, span], -1, 0),
+        ))
+    for b in range(blocks):
+        dense(cmat.at[0], b, cwt[b], ccols_ref[b : b + 1, :], OWN_ORDER)
+    wait(tables)
+    choose(1, halo_f, FAR_ORDER)
+    for b in range(blocks):
+        wait(weights[b : b + 1])
+        dense(cmat.at[1], b, cwt_f[b], ccols_f[b : b + 1, :], FAR_ORDER)
+
+    second, third, fourth, fifth = {}, {}, {}, {}
+    n = len(cuts)
+
+    def adjoint(c):
+        lo, count = cuts[c]
+        span = pl.ds(lo, count)
+        here = mine(lo, count)
+        wait(crossed[c])
+        z = [
+            zp[here] + scatter(0, [r1o[g, span] for g in range(3)]),
+            zf[span] + scatter(1, [r1f[0, span], aslot[1, here], r1f[1, span]]),
+        ]
+        z = [stacked(item) for item in z]
+        last = []
+        for t in range(2):
+            value = apply(z[t], cmat.at[t], n_own, n_slot)
+            s2[t, span] = value[:, :group]
+            loc2[t, span] = value[:, group : 2 * group]
+            s2[3 + t, span] = value[:, 2 * group : n_x]
+            last.append(value[:, n_x:])
+        s2[2, span] = blend(last[0], last[1])
+        s2[5, span] = blend(last[1], last[0])
+        second[c] = go(*[Flow(s2.at[k, span], r2.at[k, span], 1 if k < 3 else -1, 0) for k in range(6)])
+        for t in range(2):
+            bown[t, span] = apply(z[t], cmat.at[t], 0, n_own)
+
+    def middle(c):
+        lo, count = cuts[c]
+        span = pl.ds(lo, count)
+        wait(second[c])
+        slots = [
+            [r2[1, span], loc2[1, span], r2[4, span], blend(r2[2, span], r2[5, span])],
+            [r2[0, span], loc2[0, span], r2[3, span], blend(r2[5, span], r2[2, span])],
+        ]
+        last, w = [], []
+        for t in range(2):
+            w.append(stacked(bown[t, span] + scatter(t, slots[t])))
+            value = gather(t, w[t][1], 0, n_slot)
+            s3[t, span] = value[:, :group]
+            loc3[t, span] = value[:, group : 2 * group]
+            s3[3 + t, span] = value[:, 2 * group : n_x]
+            last.append(value[:, n_x:])
+        s3[2, span] = blend(last[0], last[1])
+        s3[5, span] = blend(last[1], last[0])
+        third[c] = go(*[Flow(s3.at[k, span], r3.at[k, span], -1 if k < 3 else 1, 0) for k in range(6)])
+        for t in range(2):
+            vacc[t, span] = apply_nt(w[t], cmat.at[t], 0, n_own)
+
+    def forward(c):
+        lo, count = cuts[c]
+        span = pl.ds(lo, count)
+        wait(third[c])
+        slots = [
+            [r3[1, span], loc3[1, span], r3[4, span], blend(r3[2, span], r3[5, span])],
+            [r3[0, span], loc3[0, span], r3[3, span], blend(r3[5, span], r3[2, span])],
+        ]
+        v = [None, None]
+        for t in (1, 0):
+            extra = stacked(jnp.concatenate(slots[t], axis=1))
+            v[t] = vacc[t, span] + apply_nt(extra, cmat.at[t], n_own, n_slot)
+            vacc[t, span] = v[t]
+        far_v = go(Flow(vacc.at[1, span], v_r.at[span], 0, 1))
+        value = gather(0, stacked(v[0])[1], 0, n_slot)
+        for g in range(3):
+            s4o[g, span] = value[:, g * group : (g + 1) * group]
+        s5[0, span] = value[:, n_x:]
+        far_s = go(*[Flow(s4o.at[g, span], r4x.at[g, span], g - 1, 1) for g in range(3)])
+        value = gather(1, stacked(v[1])[1], 0, n_x)
+        s4f[0, span], s4f[1, span] = value[:, :group], value[:, 2 * group :]
+        loc4[span] = value[:, group : 2 * group]
+        near = go(
+            Flow(s4f.at[0, span], r4y.at[0, span], -1, 0),
+            Flow(s4f.at[1, span], r4y.at[1, span], 1, 0),
+            Flow(s5.at[0, span], r5.at[0, 0, span], -1, 0),
+            Flow(s5.at[0, span], r5.at[1, 0, span], 1, 0),
+        )
+        fourth[c] = far_v, far_s, near
+
+    def relay(c):
+        lo, count = cuts[c]
+        span = pl.ds(lo, count)
+        wait(fourth[c][0])
+        s5[1, span] = gather(0, stacked(v_r[span])[1], n_x, group)
+        fifth[c] = go(
+            Flow(s5.at[1, span], r5.at[0, 1, span], -1, 0),
+            Flow(s5.at[1, span], r5.at[1, 1, span], 1, 0),
+        )
+
+    def finish(q, c):
+        lo, count = cuts[c]
+        span = pl.ds(lo, count)
+        if q:
+            wait(fourth[c][1])
+            wait(fifth[c])
+            pieces = [v_r[span], r4x[0, span], r4x[1, span], r4x[2, span]]
+        else:
+            wait(fourth[c][2])
+            pieces = [vacc[0, span], r4y[0, span], loc4[span], r4y[1, span]]
+        pieces.append(blend(r5[0, q, span], r5[1, q, span]))
+        both = stacked(jnp.concatenate(pieces, axis=1))
+        out_t[theirs(lo, count) if q else mine(lo, count)] = apply_nt(both, imat, 0, extent)
+
+    adjoint(0)
+    for c in range(n):
+        middle(c)
+        if c + 1 < n:
+            adjoint(c + 1)
+        forward(c)
+    for c in range(n):
+        finish(0, c)
+    for c in range(n):
+        relay(c)
+        finish(1, c)
+    for lo in range(0, feat, tile):
+        live = lax.broadcasted_iota(jnp.int32, (rows, tile), 0) < limit
+        out_ref[:, lo : lo + tile] = jnp.where(live, out_t[lo : lo + tile].T, 0.0)
+    for item in flows:
+        item.sent()
+
+
+def split(total, parts):
+    unit = total // 16
+    sizes = [16 * (unit // parts + (1 if k < unit % parts else 0)) for k in range(parts)]
+    starts = [sum(sizes[:k]) for k in range(parts)]
+    return tuple(zip(starts, sizes))
+
+
+def pair_call(n_ty, ctrl, interp_wt, interp_cols, conv_wt, conv_cols, halo_index, valid):
+    rows, feat = ctrl.shape[2:]
+    n_own = conv_wt.shape[2] * conv_wt.shape[3]
+    n_slot = halo_index.shape[2] * halo_index.shape[3]
+    extent, group, half = n_own + n_slot, n_slot // 4, feat // 2
+    cuts = split(half, 3)
+    pin = functools.partial(pltpu.with_memory_space_constraint, memory_space=pltpu.HBM)
+    hbm = pl.BlockSpec(memory_space=pltpu.HBM)
+    vmem = pl.BlockSpec(memory_space=pltpu.VMEM)
+
+    def f32(*shape):
+        return pltpu.VMEM(shape, F32)
+
+    def bf16(*shape):
+        return pltpu.VMEM(shape, BF16)
+
+    scratch = [
+        f32(rows, feat), f32(*interp_wt.shape[2:]), f32(*conv_wt.shape[2:]), f32(*conv_wt.shape[2:]),
+        pltpu.VMEM(conv_cols.shape[2:], jnp.int32), pltpu.VMEM(halo_index.shape[2:], jnp.int32),
+        bf16(2, feat, rows), bf16(2, rows, extent), bf16(2, 2, n_own, extent), bf16(2, n_own, n_slot),
+        f32(feat, n_own), f32(4, feat, group), f32(2, feat, group), f32(half, n_own),
+        f32(3, half, group), f32(2, half, group), f32(2, half, n_own),
+        f32(6, half, group), f32(6, half, group), f32(2, half, group),
+        f32(6, half, group), f32(6, half, group), f32(2, half, group), f32(2, half, n_own),
+        f32(3, half, group), f32(2, half, group), f32(half, group), f32(half, n_own),
+        f32(3, half, group), f32(2, half, group), f32(2, half, group), f32(2, 2, half, group),
+        f32(feat, rows),
+    ]
+    flows = 2 + conv_wt.shape[2] + 2 + 28 * len(cuts)
+    scratch += [pltpu.SemaphoreType.DMA((flows,))] * 2 + [pltpu.SemaphoreType.DMA((3,))]
+    return pl.pallas_call(
+        functools.partial(pair_kernel, n_ty, cuts),
+        out_shape=jax.ShapeDtypeStruct((rows, feat), F32),
+        in_specs=[pl.BlockSpec(memory_space=pltpu.SMEM), hbm, hbm, vmem, hbm, vmem, vmem],
+        out_specs=vmem,
+        scratch_shapes=scratch,
+        compiler_params=pltpu.CompilerParams(
+            collective_id=0, has_side_effects=True, vmem_limit_bytes=52 * 1024 * 1024
+        ),
+    )(
+        valid, pin(ctrl[0, 0]), pin(interp_wt[0, 0]), pin(interp_cols[0, 0]), pin(conv_wt[0, 0]),
+        pin(conv_cols[0, 0]), pin(halo_index[0, 0]),
+    )
+
+
+def pairs_fit(n_tx, ctrl, halo_index):
+    slot = halo_index.shape[3]
+    return n_tx == 2 and halo_index.shape[2] == 8 and slot == 64 and ctrl.shape[3] % 128 == 0
+
 
 def solution(mesh):
     n_ty, n_tx = mesh.shape["ty"], mesh.shape["tx"]
@@ -204,6 +583,9 @@
         n_own = conv_wt.shape[2] * conv_wt.shape[3]
         n_slot = halo_index.shape[2] * halo_index.shape[3]
         extent = n_own + n_slot
+        if pairs_fit(n_tx, ctrl, halo_index) and rows == n_own:
+            args = ctrl, interp_wt, interp_cols, conv_wt, conv_cols, halo_index, valid
+            return pair_call(n_ty, *args)[None, None]
         tiles = feat // 128
         first = 128 * max(tiles - tiles // 2, 1)
         chunks = ((0, first), (first, feat - first)) if feat > first else ((0, feat),)

time: 96.2 us -> 97.9 us (1.018)
  Pallas kernels: 93.4 us -> 95.9 us
    pallas_call x1, Pallas kernels: 93.4 us -> 95.9 us  [pair_call(): pl.pallas_call(functools.partial(pair_kernel, n_ty, cuts), out_shape=jax....]
where the time goes in v1:
time: 97.9 us; the launch traced here: 97.6 us
  Pallas kernels  95.9 us (98%)
  local copies, waits for them, and re-layouts  1.06 us (1%)
    pallas_call x1, Pallas kernels, pair_call(): pl.pallas_call(functools.partial(pair_kernel, n_ty, cuts), out_shape=jax....  95.9 us

profile of v1, /device:TPU:17, one launch (start us, length us, event | category | flops | bytes accessed | tf_op | source)
XLA Modules:
  0.0 97.6 jit_solution(15871752528430124260)
XLA Ops:
  0.7 95.9 %shard_map.73 = f32[512,640]{1,0:T(8,128)S(1)} custom-call(s32[1,1]{1,0:T(1,128)S(6)} %copy.9.valid_ref, f32[512,640]{1,0:T(8,128)} %bitcast.8, f32[4,128,384]{2,1,0:T(8,128)} %bitcast.10, s32[4,384]{1,0:T(4,128)} %bitcast.12, f32[4,128,512]{2,1,0:T(8,128)} %bitcast.9, s32[4,512]{1,0:T(4,128)} %bitcast.11, s32[8,64]{1,0:T(8,128)} %bitcast.13), custom_call_target="tpu_custom_call" | custom-call | tf_op jit(solution)/shard_map/pallas_call | solution.py:558
  96.6 1.1 %copy.10 = f32[1,1,512,640]{3,2,1,0:T(8,128)} copy(f32[1,1,512,640]{3,2,1,0:T(8,128)S(1)} %bitcast.7) | data formatting | bytes 2621440

commit v2 on v1

--- a/solution.py
+++ b/solution.py
@@ -212,8 +212,8 @@
 def pair_kernel(
     n_ty, cuts, valid_ref, ctrl_hbm, iwt_hbm, icols_ref, cwt_hbm, ccols_ref, halo_ref,
     out_ref, ctrl, iwt, cwt, cwt_f, ccols_f, halo_f, xt, imat, cmat, pick,
-    zp, aslot, r1a, zf, r1o, r1f, bown, s2, r2, loc2, s3, r3, loc3, vacc,
-    s4o, s4f, loc4, v_r, r4x, r4y, s5, r5, out_t, send_sem, recv_sem, load_sem,
+    zp, aslot, s1, r1, near, zf, r1o, bown, s2, r2, loc2, s3, r3, loc3, vacc,
+    s4o, s4f, loc4, r4o, v_r, r4x, r4y, s5, r5, out_t, send_sem, recv_sem, load_sem,
 ):
     rows, feat = ctrl.shape
     half = feat // 2
@@ -237,7 +237,7 @@
         return jnp.logical_and(ty + off >= 0, ty + off < n_ty)
 
     barrier = pltpu.get_barrier_semaphore()
-    partners = [(0, 1), (-1, 0), (1, 0), (-1, 1), (1, 1)]
+    partners = [(0, 1), (-1, 0), (1, 0)]
     for row_off, flip in partners:
         def greet(row_off=row_off, flip=flip):
             pl.semaphore_signal(
@@ -289,6 +289,15 @@
 
     def blend(first, second):
         return jnp.where(lane(first.shape[0]) < slot, first, second)
+
+    def packed(x):
+        top, low = x[: x.shape[0] // 2], x[x.shape[0] // 2 :]
+        low = pltpu.roll(low, slot, 1)
+        return blend(top, low), blend(low, top)
+
+    def unpacked(first, second):
+        low = pltpu.roll(blend(second, first), slot, 1)
+        return jnp.concatenate([blend(first, second), low], axis=0)
 
     def dense(mat, b, weights, index, order):
         where = index
@@ -334,21 +343,21 @@
     @pl.when(jnp.logical_not(there(-1)))
     def _():
         for ref in (
-            r1a.at[0], r1o.at[0], r1f.at[0], r2.at[0], r2.at[1], r2.at[2],
-            r3.at[3], r3.at[4], r3.at[5], r4x.at[2], r4y.at[1], r5.at[1],
+            r1.at[0], near.at[0], r2.at[0], r2.at[1], r2.at[2],
+            r3.at[3], r3.at[4], r3.at[5], r4o.at[1], r4y.at[1], r5.at[1],
         ):
             blank(ref)
 
     @pl.when(jnp.logical_not(there(1)))
     def _():
         for ref in (
-            r1a.at[1], r1o.at[2], r1f.at[1], r2.at[3], r2.at[4], r2.at[5],
-            r3.at[0], r3.at[1], r3.at[2], r4x.at[0], r4y.at[0], r5.at[0],
+            r1.at[1], near.at[1], r2.at[3], r2.at[4], r2.at[5],
+            r3.at[0], r3.at[1], r3.at[2], r4o.at[0], r4y.at[0], r5.at[0],
         ):
             blank(ref)
 
     loads[0].wait()
-    pl.semaphore_wait(barrier, 1 + jnp.where(there(-1), 2, 0) + jnp.where(there(1), 2, 0))
+    pl.semaphore_wait(barrier, 1 + jnp.where(there(-1), 1, 0) + jnp.where(there(1), 1, 0))
     tables = go(Flow(ccols_ref, ccols_f, 0, 1), Flow(halo_ref, halo_f, 0, 1))
     weights = go(*[Flow(cwt.at[b], cwt_f.at[b], 0, 1) for b in range(blocks)])
 
@@ -368,27 +377,29 @@
         value = apply((hi, both), imat, n_own, n_slot)
         for g in range(4):
             aslot[g, lo : lo + half] = value[:, g * group : (g + 1) * group]
-    first = go(Flow(aslot.at[3], r1a.at[0], 1, 0), Flow(aslot.at[3], r1a.at[1], -1, 0))
+    s1[0], s1[1] = packed(aslot[3])
+    first = go(Flow(s1.at[0], r1.at[0], 1, 0), Flow(s1.at[1], r1.at[1], -1, 0))
+    sides = go(Flow(aslot.at[0], near.at[0], 1, 0), Flow(aslot.at[2], near.at[1], -1, 0))
     for lo in (0, half):
         hi = xt[0, lo : lo + half]
         both = jnp.concatenate([hi, xt[1, lo : lo + half]], axis=0)
         zp[lo : lo + half] = apply((hi, both), imat, 0, n_own)
     choose(0, halo_ref, OWN_ORDER)
     wait(first)
+    extra = unpacked(r1[0], r1[1])
     for lo in (0, half):
         span = slice(lo, lo + half)
-        zp[span] = zp[span] + scatter(0, [blend(r1a[0, span], r1a[1, span])], n_x)
+        zp[span] = zp[span] + scatter(0, [extra[span]], n_x)
+    wait(sides)
     crossed = []
     for lo, count in cuts:
         span = pl.ds(lo, count)
-        away, here = theirs(lo, count), mine(lo, count)
+        away = theirs(lo, count)
         crossed.append(go(
             Flow(zp.at[away], zf.at[span], 0, 1),
+            Flow(near.at[0, away], r1o.at[0, span], 0, 1),
             Flow(aslot.at[1, away], r1o.at[1, span], 0, 1),
-            Flow(aslot.at[0, away], r1o.at[0, span], 1, 1),
-            Flow(aslot.at[2, away], r1o.at[2, span], -1, 1),
-            Flow(aslot.at[0, here], r1f.at[0, span], 1, 0),
-            Flow(aslot.at[2, here], r1f.at[1, span], -1, 0),
+            Flow(near.at[1, away], r1o.at[2, span], 0, 1),
         ))
     for b in range(blocks):
         dense(cmat.at[0], b, cwt[b], ccols_ref[b : b + 1, :], OWN_ORDER)
@@ -398,7 +409,7 @@
         wait(weights[b : b + 1])
         dense(cmat.at[1], b, cwt_f[b], ccols_f[b : b + 1, :], FAR_ORDER)
 
-    second, third, fourth, fifth = {}, {}, {}, {}
+    second, third, fourth, fifth, sixth, sides, whole = {}, {}, {}, {}, {}, {}, {}
     n = len(cuts)
 
     def adjoint(c):
@@ -408,7 +419,7 @@
         wait(crossed[c])
         z = [
             zp[here] + scatter(0, [r1o[g, span] for g in range(3)]),
-            zf[span] + scatter(1, [r1f[0, span], aslot[1, here], r1f[1, span]]),
+            zf[span] + scatter(1, [near[0, here], aslot[1, here], near[1, here]]),
         ]
         z = [stacked(item) for item in z]
         last = []
@@ -459,57 +470,73 @@
             extra = stacked(jnp.concatenate(slots[t], axis=1))
             v[t] = vacc[t, span] + apply_nt(extra, cmat.at[t], n_own, n_slot)
             vacc[t, span] = v[t]
-        far_v = go(Flow(vacc.at[1, span], v_r.at[span], 0, 1))
+        whole[c] = go(Flow(vacc.at[1, span], v_r.at[span], 0, 1))
         value = gather(0, stacked(v[0])[1], 0, n_slot)
         for g in range(3):
             s4o[g, span] = value[:, g * group : (g + 1) * group]
-        s5[0, span] = value[:, n_x:]
-        far_s = go(*[Flow(s4o.at[g, span], r4x.at[g, span], g - 1, 1) for g in range(3)])
+        sides[c] = go(
+            Flow(s4o.at[0, span], r4o.at[0, span], -1, 0), Flow(s4o.at[2, span], r4o.at[1, span], 1, 0)
+        )
+        fifth[0, c] = corner(0, c, value[:, n_x:])
         value = gather(1, stacked(v[1])[1], 0, n_x)
         s4f[0, span], s4f[1, span] = value[:, :group], value[:, 2 * group :]
         loc4[span] = value[:, group : 2 * group]
-        near = go(
-            Flow(s4f.at[0, span], r4y.at[0, span], -1, 0),
-            Flow(s4f.at[1, span], r4y.at[1, span], 1, 0),
-            Flow(s5.at[0, span], r5.at[0, 0, span], -1, 0),
-            Flow(s5.at[0, span], r5.at[1, 0, span], 1, 0),
+        fourth[c] = [
+            Flow(s4f.at[0, span], r4y.at[0, span], -1, 0), Flow(s4f.at[1, span], r4y.at[1, span], 1, 0)
+        ]
+
+    def corner(q, c, value):
+        lo, count = cuts[c]
+        span = pl.ds(lo // 2, count // 2)
+        s5[0, q, span], s5[1, q, span] = packed(value)
+        return [Flow(s5.at[0, q, span], r5.at[0, q, span], -1, 0), Flow(s5.at[1, q, span], r5.at[1, q, span], 1, 0)]
+
+    def leave(c):
+        lo, count = cuts[c]
+        span = pl.ds(lo, count)
+        wait(sides[c])
+        sixth[c] = go(
+            Flow(r4o.at[0, span], r4x.at[0, span], 0, 1),
+            Flow(s4o.at[1, span], r4x.at[1, span], 0, 1),
+            Flow(r4o.at[1, span], r4x.at[2, span], 0, 1),
         )
-        fourth[c] = far_v, far_s, near
+
+    def spare(c):
+        go(*fourth[c])
+        go(*fifth[0, c])
 
     def relay(c):
         lo, count = cuts[c]
         span = pl.ds(lo, count)
-        wait(fourth[c][0])
-        s5[1, span] = gather(0, stacked(v_r[span])[1], n_x, group)
-        fifth[c] = go(
-            Flow(s5.at[1, span], r5.at[0, 1, span], -1, 0),
-            Flow(s5.at[1, span], r5.at[1, 1, span], 1, 0),
-        )
+        wait(whole[c])
+        fifth[1, c] = corner(1, c, gather(0, stacked(v_r[span])[1], n_x, group))
+        go(*fifth[1, c])
 
     def finish(q, c):
         lo, count = cuts[c]
         span = pl.ds(lo, count)
         if q:
-            wait(fourth[c][1])
-            wait(fifth[c])
+            wait(sixth[c])
             pieces = [v_r[span], r4x[0, span], r4x[1, span], r4x[2, span]]
         else:
-            wait(fourth[c][2])
+            wait(fourth[c])
             pieces = [vacc[0, span], r4y[0, span], loc4[span], r4y[1, span]]
-        pieces.append(blend(r5[0, q, span], r5[1, q, span]))
+        wait(fifth[q, c])
+        span = pl.ds(lo // 2, count // 2)
+        pieces.append(unpacked(r5[0, q, span], r5[1, q, span]))
         both = stacked(jnp.concatenate(pieces, axis=1))
         out_t[theirs(lo, count) if q else mine(lo, count)] = apply_nt(both, imat, 0, extent)
 
-    adjoint(0)
+    for step in range(n + 3):
+        for stage, lag in ((leave, 3), (forward, 2), (middle, 1), (adjoint, 0)):
+            if 0 <= step - lag < n:
+                stage(step - lag)
     for c in range(n):
-        middle(c)
-        if c + 1 < n:
-            adjoint(c + 1)
-        forward(c)
+        spare(c)
     for c in range(n):
+        relay(c)
         finish(0, c)
     for c in range(n):
-        relay(c)
         finish(1, c)
     for lo in range(0, feat, tile):
         live = lax.broadcasted_iota(jnp.int32, (rows, tile), 0) < limit
@@ -530,7 +557,7 @@
     n_own = conv_wt.shape[2] * conv_wt.shape[3]
     n_slot = halo_index.shape[2] * halo_index.shape[3]
     extent, group, half = n_own + n_slot, n_slot // 4, feat // 2
-    cuts = split(half, 3)
+    cuts = split(half, 4)
     pin = functools.partial(pltpu.with_memory_space_constraint, memory_space=pltpu.HBM)
     hbm = pl.BlockSpec(memory_space=pltpu.HBM)
     vmem = pl.BlockSpec(memory_space=pltpu.VMEM)
@@ -545,15 +572,15 @@
         f32(rows, feat), f32(*interp_wt.shape[2:]), f32(*conv_wt.shape[2:]), f32(*conv_wt.shape[2:]),
         pltpu.VMEM(conv_cols.shape[2:], jnp.int32), pltpu.VMEM(halo_index.shape[2:], jnp.int32),
         bf16(2, feat, rows), bf16(2, rows, extent), bf16(2, 2, n_own, extent), bf16(2, n_own, n_slot),
-        f32(feat, n_own), f32(4, feat, group), f32(2, feat, group), f32(half, n_own),
-        f32(3, half, group), f32(2, half, group), f32(2, half, n_own),
+        f32(feat, n_own), f32(4, feat, group), f32(2, half, group), f32(2, half, group), f32(2, feat, group),
+        f32(half, n_own), f32(3, half, group), f32(2, half, n_own),
         f32(6, half, group), f32(6, half, group), f32(2, half, group),
         f32(6, half, group), f32(6, half, group), f32(2, half, group), f32(2, half, n_own),
-        f32(3, half, group), f32(2, half, group), f32(half, group), f32(half, n_own),
-        f32(3, half, group), f32(2, half, group), f32(2, half, group), f32(2, 2, half, group),
+        f32(3, half, group), f32(2, half, group), f32(half, group), f32(2, half, group), f32(half, n_own),
+        f32(3, half, group), f32(2, half, group), f32(2, 2, half // 2, group), f32(2, 2, half // 2, group),
         f32(feat, rows),
     ]
-    flows = 2 + conv_wt.shape[2] + 2 + 28 * len(cuts)
+    flows = 2 + conv_wt.shape[2] + 4 + 28 * len(cuts)
     scratch += [pltpu.SemaphoreType.DMA((flows,))] * 2 + [pltpu.SemaphoreType.DMA((3,))]
     return pl.pallas_call(
         functools.partial(pair_kernel, n_ty, cuts),

time: 97.9 us -> 86.9 us (0.89)
  Pallas kernels: 95.9 us -> 84.6 us
    pallas_call x1, Pallas kernels: 95.9 us -> 84.6 us  [pair_call(): pl.pallas_call(functools.partial(pair_kernel, n_ty, cuts), out_shape=jax....]
where the time goes in v2:
time: 86.9 us; the launch traced here: 86.3 us
  Pallas kernels  84.6 us (97%)
  local copies, waits for them, and re-layouts  1.06 us (1%)
    pallas_call x1, Pallas kernels, pair_call(): pl.pallas_call(functools.partial(pair_kernel, n_ty, cuts), out_shape=jax....  84.6 us

profile of v2, /device:TPU:17, one launch (start us, length us, event | category | flops | bytes accessed | tf_op | source)
XLA Modules:
  0.0 86.3 jit_solution(17203504244185323756)
XLA Ops:
  0.7 84.6 %shard_map.73 = f32[512,640]{1,0:T(8,128)S(1)} custom-call(s32[1,1]{1,0:T(1,128)S(6)} %copy.9.valid_ref, f32[512,640]{1,0:T(8,128)} %bitcast.8, f32[4,128,384]{2,1,0:T(8,128)} %bitcast.10, s32[4,384]{1,0:T(4,128)} %bitcast.12, f32[4,128,512]{2,1,0:T(8,128)} %bitcast.9, s32[4,512]{1,0:T(4,128)} %bitcast.11, s32[8,64]{1,0:T(8,128)} %bitcast.13), custom_call_target="tpu_custom_call" | custom-call | tf_op jit(solution)/shard_map/pallas_call | solution.py:585
  85.2 1.1 %copy.10 = f32[1,1,512,640]{3,2,1,0:T(8,128)} copy(f32[1,1,512,640]{3,2,1,0:T(8,128)S(1)} %bitcast.7) | data formatting | bytes 2621440

commit v3 on v2

--- a/solution.py
+++ b/solution.py
@@ -210,10 +210,10 @@
 
 
 def pair_kernel(
-    n_ty, cuts, valid_ref, ctrl_hbm, iwt_hbm, icols_ref, cwt_hbm, ccols_ref, halo_ref,
-    out_ref, ctrl, iwt, cwt, cwt_f, ccols_f, halo_f, xt, imat, cmat, pick,
-    zp, aslot, s1, r1, near, zf, r1o, bown, s2, r2, loc2, s3, r3, loc3, vacc,
-    s4o, s4f, loc4, r4o, v_r, r4x, r4y, s5, r5, out_t, send_sem, recv_sem, load_sem,
+    n_ty, cuts, valid_ref, ctrl_hbm, iwt_hbm, icols_hbm, cwt_hbm, ccols_hbm, halo_hbm,
+    out_ref, icols_ref, ccols_ref, halo_ref, ctrl, iwt, cwt, cwt_f, ccols_f, halo_f, xt, imat, cmat, pick,
+    zp, s1, near, zf, r1o, bown, s2, r2, loc2, s3, r3, loc3, vacc,
+    s4o, r4o, r4x, v_r, s6, r6, loc6, s5, r5, out_t, out_v, send_sem, recv_sem, load_sem, store_sem,
 ):
     rows, feat = ctrl.shape
     half = feat // 2
@@ -229,6 +229,9 @@
         pltpu.make_async_copy(cwt_hbm, cwt, load_sem.at[0]),
         pltpu.make_async_copy(iwt_hbm, iwt, load_sem.at[1]),
         pltpu.make_async_copy(ctrl_hbm, ctrl, load_sem.at[2]),
+        pltpu.make_async_copy(icols_hbm, icols_ref, load_sem.at[3]),
+        pltpu.make_async_copy(ccols_hbm, ccols_ref, load_sem.at[4]),
+        pltpu.make_async_copy(halo_hbm, halo_ref, load_sem.at[5]),
     ]
     for item in loads:
         item.start()
@@ -248,17 +251,18 @@
         else:
             greet()
 
-    flows = []
+    flows, tags = [], {}
 
     class Flow:
-        def __init__(self, src, dst, row_off, flip):
+        def __init__(self, src, dst, row_off, flip, tag=None):
             self.row_off = row_off
-            self.key = len(flows)
-            flows.append(self)
+            self.tag = tag or len(flows)
+            key = tags.setdefault(self.tag, [len(tags), None])[0]
             self.copy = pltpu.make_async_remote_copy(
-                src_ref=src, dst_ref=dst, send_sem=send_sem.at[self.key], recv_sem=recv_sem.at[self.key],
+                src_ref=src, dst_ref=dst, send_sem=send_sem.at[key], recv_sem=recv_sem.at[len(flows)],
                 device_id=(ty + row_off, far if flip else tx), device_id_type=MESH,
             )
+            flows.append(self)
 
         def act(self, sign, action):
             if self.row_off:
@@ -267,6 +271,10 @@
                 action()
 
         def start(self):
+            before = tags[self.tag][1]
+            if before is not None:
+                before.sent()
+            tags[self.tag][1] = self
             self.act(1, lambda: self.copy.start())
 
         def arrived(self):
@@ -317,8 +325,8 @@
         pick[t] = hot.astype(F32).astype(BF16)
 
     def scatter(t, pieces, lo=0):
-        _, both = stacked(jnp.concatenate(pieces, axis=1) if len(pieces) > 1 else pieces[0])
-        return folded(dot_nt(both, pick[t, :, lo : lo + group * len(pieces)]))
+        value = jnp.concatenate(pieces, axis=1) if len(pieces) > 1 else pieces[0]
+        return folded(dot_nt(stacked(value)[1], pick[t, :, lo : lo + value.shape[1]]))
 
     def apply(x, mat, lo, count):
         hi, both = x
@@ -331,35 +339,39 @@
     def gather(t, both, lo, count):
         return folded(dot(both, pick[t, :, lo : lo + count]))
 
+    def within(side, lo, count):
+        start = side * lo + (1 - side) * (half - lo - count)
+        return pl.ds(pl.multiple_of(start, 16), count)
+
+    def placed(side, lo, count):
+        start = side * (half + lo) + (1 - side) * (half - lo - count)
+        return pl.ds(pl.multiple_of(start, 16), count)
+
     def mine(lo, count):
-        return pl.ds(pl.multiple_of(tx * half + lo, 16), count)
+        return placed(tx, lo, count)
 
     def theirs(lo, count):
-        return pl.ds(pl.multiple_of(far * half + lo, 16), count)
+        return placed(far, lo, count)
 
     def blank(ref):
         ref[...] = jnp.zeros(ref.shape, ref.dtype)
 
     @pl.when(jnp.logical_not(there(-1)))
     def _():
-        for ref in (
-            r1.at[0], near.at[0], r2.at[0], r2.at[1], r2.at[2],
-            r3.at[3], r3.at[4], r3.at[5], r4o.at[1], r4y.at[1], r5.at[1],
-        ):
+        for ref in (near.at[0], r2.at[0], r3.at[1], r4o.at[2], r6.at[1], r5.at[1]):
             blank(ref)
 
     @pl.when(jnp.logical_not(there(1)))
     def _():
-        for ref in (
-            r1.at[1], near.at[1], r2.at[3], r2.at[4], r2.at[5],
-            r3.at[0], r3.at[1], r3.at[2], r4o.at[0], r4y.at[0], r5.at[0],
-        ):
+        for ref in (near.at[2], r2.at[1], r3.at[0], r4o.at[0], r6.at[0], r5.at[0]):
             blank(ref)
 
     loads[0].wait()
     pl.semaphore_wait(barrier, 1 + jnp.where(there(-1), 1, 0) + jnp.where(there(1), 1, 0))
+    for item in loads[3:]:
+        item.wait()
     tables = go(Flow(ccols_ref, ccols_f, 0, 1), Flow(halo_ref, halo_f, 0, 1))
-    weights = go(*[Flow(cwt.at[b], cwt_f.at[b], 0, 1) for b in range(blocks)])
+    weights = go(Flow(cwt, cwt_f, 0, 1))
 
     limit = valid_ref[0, 0]
     loads[1].wait()
@@ -371,178 +383,196 @@
         live = lax.broadcasted_iota(jnp.int32, (rows, tile), 0) < limit
         piece = jnp.where(live, ctrl[:, lo : lo + tile], 0.0).T
         xt[0, lo : lo + tile], xt[1, lo : lo + tile] = halves(piece)
-    for lo in (0, half):
-        hi = xt[0, lo : lo + half]
-        both = jnp.concatenate([hi, xt[1, lo : lo + half]], axis=0)
-        value = apply((hi, both), imat, n_own, n_slot)
-        for g in range(4):
-            aslot[g, lo : lo + half] = value[:, g * group : (g + 1) * group]
-    s1[0], s1[1] = packed(aslot[3])
-    first = go(Flow(s1.at[0], r1.at[0], 1, 0), Flow(s1.at[1], r1.at[1], -1, 0))
-    sides = go(Flow(aslot.at[0], near.at[0], 1, 0), Flow(aslot.at[2], near.at[1], -1, 0))
-    for lo in (0, half):
-        hi = xt[0, lo : lo + half]
-        both = jnp.concatenate([hi, xt[1, lo : lo + half]], axis=0)
-        zp[lo : lo + half] = apply((hi, both), imat, 0, n_own)
+    last = []
+    for q in range(2):
+        span = slice(q * half, (q + 1) * half)
+        both = jnp.concatenate([xt[0, span], xt[1, span]], axis=0)
+        value = apply((xt[0, span], both), imat, n_own, n_slot)
+        s1[0, q], near[1, q], s1[1, q] = (value[:, g * group : (g + 1) * group] for g in range(3))
+        last.append(value[:, n_x:])
+    s1[0, 2], s1[1, 2] = packed(jnp.concatenate(last, axis=0))
+    first = go(Flow(s1.at[0], near.at[0], 1, 0), Flow(s1.at[1], near.at[2], -1, 0))
+    for q in range(2):
+        span = slice(q * half, (q + 1) * half)
+        both = jnp.concatenate([xt[0, span], xt[1, span]], axis=0)
+        zp[span] = apply((xt[0, span], both), imat, 0, n_own)
     choose(0, halo_ref, OWN_ORDER)
     wait(first)
-    extra = unpacked(r1[0], r1[1])
-    for lo in (0, half):
-        span = slice(lo, lo + half)
+    extra = unpacked(near[0, 2], near[2, 2])
+    for q in range(2):
+        span = slice(q * half, (q + 1) * half)
         zp[span] = zp[span] + scatter(0, [extra[span]], n_x)
-    wait(sides)
     crossed = []
     for lo, count in cuts:
         span = pl.ds(lo, count)
-        away = theirs(lo, count)
         crossed.append(go(
-            Flow(zp.at[away], zf.at[span], 0, 1),
-            Flow(near.at[0, away], r1o.at[0, span], 0, 1),
-            Flow(aslot.at[1, away], r1o.at[1, span], 0, 1),
-            Flow(near.at[1, away], r1o.at[2, span], 0, 1),
+            Flow(zp.at[theirs(lo, count)], zf.at[span], 0, 1),
+            Flow(near.at[:, far, within(far, lo, count)], r1o.at[:, span], 0, 1),
         ))
     for b in range(blocks):
         dense(cmat.at[0], b, cwt[b], ccols_ref[b : b + 1, :], OWN_ORDER)
     wait(tables)
     choose(1, halo_f, FAR_ORDER)
+    wait(weights)
     for b in range(blocks):
-        wait(weights[b : b + 1])
         dense(cmat.at[1], b, cwt_f[b], ccols_f[b : b + 1, :], FAR_ORDER)
 
     second, third, fourth, fifth, sixth, sides, whole = {}, {}, {}, {}, {}, {}, {}
     n = len(cuts)
+
+    def swap(c, sent, got, kept, sign, tag, value):
+        span = pl.ds(*cuts[c])
+        last = []
+        for t in range(2):
+            sent[0, t, span], kept[t, span] = value[t][:, :group], value[t][:, group : 2 * group]
+            sent[1, t, span] = value[t][:, 2 * group : n_x]
+            last.append(value[t][:, n_x:])
+        sent[0, 2, span], sent[1, 2, span] = blend(last[0], last[1]), blend(last[1], last[0])
+        return go(*[
+            Flow(sent.at[k, :, span], got.at[k, :, span], sign - 2 * k * sign, 0, (tag, k)) for k in range(2)
+        ])
+
+    def swapped(c, got, kept):
+        span = pl.ds(*cuts[c])
+        return [
+            jnp.concatenate([
+                got[0, 1 - t, span], kept[1 - t, span], got[1, 1 - t, span],
+                blend(got[t, 2, span], got[1 - t, 2, span]),
+            ], axis=1)
+            for t in range(2)
+        ]
 
     def adjoint(c):
         lo, count = cuts[c]
         span = pl.ds(lo, count)
-        here = mine(lo, count)
+        here = within(tx, lo, count)
         wait(crossed[c])
         z = [
-            zp[here] + scatter(0, [r1o[g, span] for g in range(3)]),
-            zf[span] + scatter(1, [near[0, here], aslot[1, here], near[1, here]]),
+            zp[mine(lo, count)] + scatter(0, [r1o[g, span] for g in range(3)]),
+            zf[span] + scatter(1, [near[g, tx, here] for g in range(3)]),
         ]
         z = [stacked(item) for item in z]
-        last = []
-        for t in range(2):
-            value = apply(z[t], cmat.at[t], n_own, n_slot)
-            s2[t, span] = value[:, :group]
-            loc2[t, span] = value[:, group : 2 * group]
-            s2[3 + t, span] = value[:, 2 * group : n_x]
-            last.append(value[:, n_x:])
-        s2[2, span] = blend(last[0], last[1])
-        s2[5, span] = blend(last[1], last[0])
-        second[c] = go(*[Flow(s2.at[k, span], r2.at[k, span], 1 if k < 3 else -1, 0) for k in range(6)])
+        second[c] = swap(c, s2, r2, loc2, 1, "b", [apply(z[t], cmat.at[t], n_own, n_slot) for t in range(2)])
         for t in range(2):
             bown[t, span] = apply(z[t], cmat.at[t], 0, n_own)
 
     def middle(c):
-        lo, count = cuts[c]
-        span = pl.ds(lo, count)
+        span = pl.ds(*cuts[c])
         wait(second[c])
-        slots = [
-            [r2[1, span], loc2[1, span], r2[4, span], blend(r2[2, span], r2[5, span])],
-            [r2[0, span], loc2[0, span], r2[3, span], blend(r2[5, span], r2[2, span])],
-        ]
-        last, w = [], []
-        for t in range(2):
-            w.append(stacked(bown[t, span] + scatter(t, slots[t])))
-            value = gather(t, w[t][1], 0, n_slot)
-            s3[t, span] = value[:, :group]
-            loc3[t, span] = value[:, group : 2 * group]
-            s3[3 + t, span] = value[:, 2 * group : n_x]
-            last.append(value[:, n_x:])
-        s3[2, span] = blend(last[0], last[1])
-        s3[5, span] = blend(last[1], last[0])
-        third[c] = go(*[Flow(s3.at[k, span], r3.at[k, span], -1 if k < 3 else 1, 0) for k in range(6)])
+        slots = swapped(c, r2, loc2)
+        w = [stacked(bown[t, span] + scatter(t, [slots[t]])) for t in range(2)]
+        third[c] = swap(c, s3, r3, loc3, -1, "w", [gather(t, w[t][1], 0, n_slot) for t in range(2)])
         for t in range(2):
             vacc[t, span] = apply_nt(w[t], cmat.at[t], 0, n_own)
 
     def forward(c):
         lo, count = cuts[c]
-        span = pl.ds(lo, count)
+        span, part = pl.ds(lo, count), pl.ds(lo // 2, count // 2)
         wait(third[c])
-        slots = [
-            [r3[1, span], loc3[1, span], r3[4, span], blend(r3[2, span], r3[5, span])],
-            [r3[0, span], loc3[0, span], r3[3, span], blend(r3[5, span], r3[2, span])],
-        ]
+        slots = swapped(c, r3, loc3)
         v = [None, None]
         for t in (1, 0):
-            extra = stacked(jnp.concatenate(slots[t], axis=1))
-            v[t] = vacc[t, span] + apply_nt(extra, cmat.at[t], n_own, n_slot)
+            v[t] = vacc[t, span] + apply_nt(stacked(slots[t]), cmat.at[t], n_own, n_slot)
             vacc[t, span] = v[t]
-        whole[c] = go(Flow(vacc.at[1, span], v_r.at[span], 0, 1))
+            if t:
+                whole[c] = go(Flow(vacc.at[1, span], v_r.at[span], 0, 1))
         value = gather(0, stacked(v[0])[1], 0, n_slot)
-        for g in range(3):
-            s4o[g, span] = value[:, g * group : (g + 1) * group]
+        s4o[0, span], r4o[1, span], s4o[1, span] = (value[:, g * group : (g + 1) * group] for g in range(3))
         sides[c] = go(
-            Flow(s4o.at[0, span], r4o.at[0, span], -1, 0), Flow(s4o.at[2, span], r4o.at[1, span], 1, 0)
+            Flow(s4o.at[0, span], r4o.at[0, span], -1, 0, ("s", 0)),
+            Flow(s4o.at[1, span], r4o.at[2, span], 1, 0, ("s", 1)),
         )
-        fifth[0, c] = corner(0, c, value[:, n_x:])
+        s6[0, 2, part], s6[1, 2, part] = packed(value[:, n_x:])
         value = gather(1, stacked(v[1])[1], 0, n_x)
-        s4f[0, span], s4f[1, span] = value[:, :group], value[:, 2 * group :]
-        loc4[span] = value[:, group : 2 * group]
-        fourth[c] = [
-            Flow(s4f.at[0, span], r4y.at[0, span], -1, 0), Flow(s4f.at[1, span], r4y.at[1, span], 1, 0)
-        ]
-
-    def corner(q, c, value):
+        loc6[span] = value[:, group : 2 * group]
+        for q in range(2):
+            rows_q = slice(q * (count // 2), (q + 1) * (count // 2))
+            s6[0, q, part], s6[1, q, part] = value[rows_q, :group], value[rows_q, 2 * group :]
+
+    def leave(c):
+        span = pl.ds(*cuts[c])
+        wait(sides[c])
+        sixth[c] = go(Flow(r4o.at[:, span], r4x.at[:, span], 0, 1))
+
+    def spare(c):
         lo, count = cuts[c]
-        span = pl.ds(lo // 2, count // 2)
-        s5[0, q, span], s5[1, q, span] = packed(value)
-        return [Flow(s5.at[0, q, span], r5.at[0, q, span], -1, 0), Flow(s5.at[1, q, span], r5.at[1, q, span], 1, 0)]
-
-    def leave(c):
-        lo, count = cuts[c]
-        span = pl.ds(lo, count)
-        wait(sides[c])
-        sixth[c] = go(
-            Flow(r4o.at[0, span], r4x.at[0, span], 0, 1),
-            Flow(s4o.at[1, span], r4x.at[1, span], 0, 1),
-            Flow(r4o.at[1, span], r4x.at[2, span], 0, 1),
-        )
-
-    def spare(c):
-        go(*fourth[c])
-        go(*fifth[0, c])
+        part = pl.ds(lo // 2, count // 2)
+        fourth[c] = go(*[
+            Flow(s6.at[k, :, part], r6.at[k, :, part], 2 * k - 1, 0, ("n", k)) for k in range(2)
+        ])
 
     def relay(c):
         lo, count = cuts[c]
-        span = pl.ds(lo, count)
+        part = pl.ds(lo // 2, count // 2)
         wait(whole[c])
-        fifth[1, c] = corner(1, c, gather(0, stacked(v_r[span])[1], n_x, group))
-        go(*fifth[1, c])
-
-    def finish(q, c):
+        s5[0, part], s5[1, part] = packed(gather(0, stacked(v_r[pl.ds(lo, count)])[1], n_x, group))
+        fifth[c] = go(*[Flow(s5.at[k, part], r5.at[k, part], 2 * k - 1, 0, ("c", k)) for k in range(2)])
+
+    def finish(q, c, stages=(0, 1)):
         lo, count = cuts[c]
-        span = pl.ds(lo, count)
-        if q:
+        span, part = pl.ds(lo, count), pl.ds(lo // 2, count // 2)
+        place = theirs(lo, count) if q else mine(lo, count)
+        if 0 in stages:
+            wait(fifth[c] if q else fourth[c])
+            last = unpacked(r5[0, part], r5[1, part]) if q else unpacked(r6[0, 2, part], r6[1, 2, part])
+            main = v_r[span] if q else vacc[0, span]
+        if 1 in stages and q:
             wait(sixth[c])
-            pieces = [v_r[span], r4x[0, span], r4x[1, span], r4x[2, span]]
+            outer = [r4x[g, span] for g in range(3)]
+        elif 1 in stages:
+            outer = [jnp.concatenate([r6[k, 0, part], r6[k, 1, part]], axis=0) for k in range(2)]
+            outer.insert(1, loc6[span])
+        if len(stages) == 2:
+            both = stacked(jnp.concatenate([main, *outer, last], axis=1))
+            out_t[place] = apply_nt(both, imat, 0, extent)
+        elif 0 in stages:
+            out_t[place] = apply_nt(stacked(main), imat, 0, n_own) + apply_nt(stacked(last), imat, n_own + n_x, group)
         else:
-            wait(fourth[c])
-            pieces = [vacc[0, span], r4y[0, span], loc4[span], r4y[1, span]]
-        wait(fifth[q, c])
-        span = pl.ds(lo // 2, count // 2)
-        pieces.append(unpacked(r5[0, q, span], r5[1, q, span]))
-        both = stacked(jnp.concatenate(pieces, axis=1))
-        out_t[theirs(lo, count) if q else mine(lo, count)] = apply_nt(both, imat, 0, extent)
+            both = stacked(jnp.concatenate(outer, axis=1))
+            out_t[place] = out_t[place] + apply_nt(both, imat, n_own, n_x)
+
+    stores = []
+
+    def ready(r):
+        return max([c for c in range(n) if half + cuts[c][0] < (r + 1) * tile], default=-1)
+
+    def store(c):
+        for r in range(feat // tile):
+            if ready(r) == c:
+                block = far * r + tx * (feat // tile - 1 - r)
+                span = pl.ds(pl.multiple_of(block * tile, tile), tile)
+                live = lax.broadcasted_iota(jnp.int32, (rows, tile), 0) < limit
+                out_v[r] = jnp.where(live, out_t[span].T, 0.0)
+                stores.append(pltpu.make_async_copy(out_v.at[r], out_ref.at[:, span], store_sem.at[r]))
+                stores[-1].start()
 
     for step in range(n + 3):
         for stage, lag in ((leave, 3), (forward, 2), (middle, 1), (adjoint, 0)):
             if 0 <= step - lag < n:
                 stage(step - lag)
-    for c in range(n):
-        spare(c)
-    for c in range(n):
-        relay(c)
-        finish(0, c)
-    for c in range(n):
+        if step == n + 1:
+            for c in range(n - 2):
+                relay(c)
+                finish(0, c)
+        if 0 <= step - 2 < n:
+            spare(step - 2)
+    relay(n - 2)
+    finish(0, n - 2)
+    for c in range(n - 2):
         finish(1, c)
-    for lo in range(0, feat, tile):
-        live = lax.broadcasted_iota(jnp.int32, (rows, tile), 0) < limit
-        out_ref[:, lo : lo + tile] = jnp.where(live, out_t[lo : lo + tile].T, 0.0)
-    for item in flows:
+    relay(n - 1)
+    finish(0, n - 1)
+    for c in range(-1, n - 2):
+        store(c)
+    finish(1, n - 2)
+    store(n - 2)
+    finish(1, n - 1, (0,))
+    finish(1, n - 1, (1,))
+    store(n - 1)
+    for _, item in tags.values():
         item.sent()
+    for item in stores:
+        item.wait()
 
 
 def split(total, parts):
@@ -569,24 +599,26 @@
         return pltpu.VMEM(shape, BF16)
 
     scratch = [
+        *[pltpu.VMEM(item.shape[2:], jnp.int32) for item in (interp_cols, conv_cols, halo_index)],
         f32(rows, feat), f32(*interp_wt.shape[2:]), f32(*conv_wt.shape[2:]), f32(*conv_wt.shape[2:]),
         pltpu.VMEM(conv_cols.shape[2:], jnp.int32), pltpu.VMEM(halo_index.shape[2:], jnp.int32),
         bf16(2, feat, rows), bf16(2, rows, extent), bf16(2, 2, n_own, extent), bf16(2, n_own, n_slot),
-        f32(feat, n_own), f32(4, feat, group), f32(2, half, group), f32(2, half, group), f32(2, feat, group),
+        f32(feat, n_own), f32(2, 3, half, group), f32(3, 3, half, group),
         f32(half, n_own), f32(3, half, group), f32(2, half, n_own),
-        f32(6, half, group), f32(6, half, group), f32(2, half, group),
-        f32(6, half, group), f32(6, half, group), f32(2, half, group), f32(2, half, n_own),
-        f32(3, half, group), f32(2, half, group), f32(half, group), f32(2, half, group), f32(half, n_own),
-        f32(3, half, group), f32(2, half, group), f32(2, 2, half // 2, group), f32(2, 2, half // 2, group),
-        f32(feat, rows),
+        f32(2, 3, half, group), f32(2, 3, half, group), f32(2, half, group),
+        f32(2, 3, half, group), f32(2, 3, half, group), f32(2, half, group), f32(2, half, n_own),
+        f32(2, half, group), f32(3, half, group), f32(3, half, group), f32(half, n_own),
+        f32(2, 3, half // 2, group), f32(2, 3, half // 2, group), f32(half, group),
+        f32(2, half // 2, group), f32(2, half // 2, group),
+        f32(feat, rows), f32(feat // 128, rows, 128),
     ]
-    flows = 2 + conv_wt.shape[2] + 4 + 28 * len(cuts)
-    scratch += [pltpu.SemaphoreType.DMA((flows,))] * 2 + [pltpu.SemaphoreType.DMA((3,))]
+    dma = pltpu.SemaphoreType.DMA
+    scratch += [dma((15 + 4 * len(cuts),)), dma((5 + 14 * len(cuts),)), dma((6,)), dma((feat // 128,))]
     return pl.pallas_call(
         functools.partial(pair_kernel, n_ty, cuts),
         out_shape=jax.ShapeDtypeStruct((rows, feat), F32),
-        in_specs=[pl.BlockSpec(memory_space=pltpu.SMEM), hbm, hbm, vmem, hbm, vmem, vmem],
-        out_specs=vmem,
+        in_specs=[pl.BlockSpec(memory_space=pltpu.SMEM)] + [hbm] * 6,
+        out_specs=pl.BlockSpec(memory_space=pl.ANY),
         scratch_shapes=scratch,
         compiler_params=pltpu.CompilerParams(
             collective_id=0, has_side_effects=True, vmem_limit_bytes=52 * 1024 * 1024

time: 86.9 us -> 83.7 us (0.963)
  Pallas kernels: 84.6 us -> 81.8 us
    pallas_call x1, Pallas kernels: 84.6 us -> 81.8 us  [pair_call(): pl.pallas_call(functools.partial(pair_kernel, n_ty, cuts), out_shape=jax....]
where the time goes in v3:
time: 83.7 us; the launch traced here: 83.5 us
  Pallas kernels  81.8 us (98%)
  local copies, waits for them, and re-layouts  1.06 us (1%)
    pallas_call x1, Pallas kernels, pair_call(): pl.pallas_call(functools.partial(pair_kernel, n_ty, cuts), out_shape=jax....  81.8 us

profile of v3, /device:TPU:17, one launch (start us, length us, event | category | flops | bytes accessed | tf_op | source)
XLA Modules:
  0.0 83.5 jit_solution(5170189892768187880)
XLA Ops:
  0.7 81.8 %shard_map.73 = f32[512,640]{1,0:T(8,128)S(1)} custom-call(s32[1,1]{1,0:T(1,128)S(6)} %copy.9.valid_ref, f32[512,640]{1,0:T(8,128)} %bitcast.8, f32[4,128,384]{2,1,0:T(8,128)} %bitcast.10, s32[4,384]{1,0:T(4,128)} %bitcast.12, f32[4,128,512]{2,1,0:T(8,128)} %bitcast.9, s32[4,512]{1,0:T(4,128)} %bitcast.11, s32[8,64]{1,0:T(8,128)} %bitcast.13), custom_call_target="tpu_custom_call" | custom-call | tf_op jit(solution)/shard_map/pallas_call | solution.py:617
  82.5 1.1 %copy.10 = f32[1,1,512,640]{3,2,1,0:T(8,128)} copy(f32[1,1,512,640]{3,2,1,0:T(8,128)S(1)} %bitcast.7) | data formatting | bytes 2621440

commit v4 on v3

--- a/solution.py
+++ b/solution.py
@@ -211,7 +211,7 @@
 
 def pair_kernel(
     n_ty, cuts, valid_ref, ctrl_hbm, iwt_hbm, icols_hbm, cwt_hbm, ccols_hbm, halo_hbm,
-    out_ref, icols_ref, ccols_ref, halo_ref, ctrl, iwt, cwt, cwt_f, ccols_f, halo_f, xt, imat, cmat, pick,
+    out_ref, icols_ref, ccols_ref, halo_ref, ctrl, iwt, cwt, cwt_f, ccols_f, halo_f, xt, imat, imat_t, cmat, cmat_t, pick, pick_t,
     zp, s1, near, zf, r1o, bown, s2, r2, loc2, s3, r3, loc3, vacc,
     s4o, r4o, r4x, v_r, s6, r6, loc6, s5, r5, out_t, out_v, send_sem, recv_sem, load_sem, store_sem,
 ):
@@ -307,7 +307,7 @@
         low = pltpu.roll(blend(second, first), slot, 1)
         return jnp.concatenate([blend(first, second), low], axis=0)
 
-    def dense(mat, b, weights, index, order):
+    def dense(mat, mat_t, b, weights, index, order):
         where = index
         for place, d in enumerate(order):
             low = n_own + d * slot
@@ -317,24 +317,28 @@
         hot = lax.broadcasted_iota(jnp.int32, (extent, width), 0) == where
         _, both = stacked(weights)
         span = pl.ds(b * height, height)
-        mat[0, span], mat[1, span] = halves(folded(dot_nt(both, hot.astype(F32).astype(BF16))))
+        hot = hot.astype(F32).astype(BF16)
+        mat[0, span], mat[1, span] = halves(folded(dot_nt(both, hot)))
+        turned = dot_nt(hot, both)
+        mat_t[0, :, span], mat_t[1, :, span] = halves(turned[:, :height] + turned[:, height:])
 
     def choose(t, ref, order):
         halo = jnp.concatenate([ref[d : d + 1, :] for d in order], axis=1)
         hot = lax.broadcasted_iota(jnp.int32, (n_own, n_slot), 0) == halo
-        pick[t] = hot.astype(F32).astype(BF16)
+        hot = hot.astype(F32)
+        pick[t], pick_t[t] = hot.astype(BF16), hot.T.astype(BF16)
 
     def scatter(t, pieces, lo=0):
         value = jnp.concatenate(pieces, axis=1) if len(pieces) > 1 else pieces[0]
-        return folded(dot_nt(stacked(value)[1], pick[t, :, lo : lo + value.shape[1]]))
+        return folded(dot(stacked(value)[1], pick_t[t, lo : lo + value.shape[1]]))
 
     def apply(x, mat, lo, count):
         hi, both = x
         return folded(dot(both, mat[0, :, lo : lo + count])) + dot(hi, mat[1, :, lo : lo + count])
 
-    def apply_nt(x, mat, lo, count):
+    def apply_t(x, mat, lo, count):
         hi, both = x
-        return folded(dot_nt(both, mat[0, :, lo : lo + count])) + dot_nt(hi, mat[1, :, lo : lo + count])
+        return folded(dot(both, mat[0, lo : lo + count])) + dot(hi, mat[1, lo : lo + count])
 
     def gather(t, both, lo, count):
         return folded(dot(both, pick[t, :, lo : lo + count]))
@@ -376,7 +380,7 @@
     limit = valid_ref[0, 0]
     loads[1].wait()
     for b in range(iwt.shape[0]):
-        dense(imat, b, iwt[b], icols_ref[b : b + 1, :], OWN_ORDER)
+        dense(imat, imat_t, b, iwt[b], icols_ref[b : b + 1, :], OWN_ORDER)
     loads[2].wait()
     tile = 128
     for lo in range(0, feat, tile):
@@ -410,12 +414,12 @@
             Flow(near.at[:, far, within(far, lo, count)], r1o.at[:, span], 0, 1),
         ))
     for b in range(blocks):
-        dense(cmat.at[0], b, cwt[b], ccols_ref[b : b + 1, :], OWN_ORDER)
+        dense(cmat.at[0], cmat_t.at[0], b, cwt[b], ccols_ref[b : b + 1, :], OWN_ORDER)
     wait(tables)
     choose(1, halo_f, FAR_ORDER)
     wait(weights)
     for b in range(blocks):
-        dense(cmat.at[1], b, cwt_f[b], ccols_f[b : b + 1, :], FAR_ORDER)
+        dense(cmat.at[1], cmat_t.at[1], b, cwt_f[b], ccols_f[b : b + 1, :], FAR_ORDER)
 
     second, third, fourth, fifth, sixth, sides, whole = {}, {}, {}, {}, {}, {}, {}
     n = len(cuts)
@@ -463,7 +467,7 @@
         w = [stacked(bown[t, span] + scatter(t, [slots[t]])) for t in range(2)]
         third[c] = swap(c, s3, r3, loc3, -1, "w", [gather(t, w[t][1], 0, n_slot) for t in range(2)])
         for t in range(2):
-            vacc[t, span] = apply_nt(w[t], cmat.at[t], 0, n_own)
+            vacc[t, span] = apply_t(w[t], cmat_t.at[t], 0, n_own)
 
     def forward(c):
         lo, count = cuts[c]
@@ -472,7 +476,7 @@
         slots = swapped(c, r3, loc3)
         v = [None, None]
         for t in (1, 0):
-            v[t] = vacc[t, span] + apply_nt(stacked(slots[t]), cmat.at[t], n_own, n_slot)
+            v[t] = vacc[t, span] + apply_t(stacked(slots[t]), cmat_t.at[t], n_own, n_slot)
             vacc[t, span] = v[t]
             if t:
                 whole[c] = go(Flow(vacc.at[1, span], v_r.at[span], 0, 1))
@@ -498,7 +502,7 @@
         lo, count = cuts[c]
         part = pl.ds(lo // 2, count // 2)
         fourth[c] = go(*[
-            Flow(s6.at[k, :, part], r6.at[k, :, part], 2 * k - 1, 0, ("n", k)) for k in range(2)
+            Flow(s6.at[k, :, part], r6.at[k, :, part], 2 * k - 1, 0) for k in range(2)
         ])
 
     def relay(c):
@@ -506,7 +510,7 @@
         part = pl.ds(lo // 2, count // 2)
         wait(whole[c])
         s5[0, part], s5[1, part] = packed(gather(0, stacked(v_r[pl.ds(lo, count)])[1], n_x, group))
-        fifth[c] = go(*[Flow(s5.at[k, part], r5.at[k, part], 2 * k - 1, 0, ("c", k)) for k in range(2)])
+        fifth[c] = go(*[Flow(s5.at[k, part], r5.at[k, part], 2 * k - 1, 0) for k in range(2)])
 
     def finish(q, c, stages=(0, 1)):
         lo, count = cuts[c]
@@ -524,12 +528,12 @@
             outer.insert(1, loc6[span])
         if len(stages) == 2:
             both = stacked(jnp.concatenate([main, *outer, last], axis=1))
-            out_t[place] = apply_nt(both, imat, 0, extent)
+            out_t[place] = apply_t(both, imat_t, 0, extent)
         elif 0 in stages:
-            out_t[place] = apply_nt(stacked(main), imat, 0, n_own) + apply_nt(stacked(last), imat, n_own + n_x, group)
+            out_t[place] = apply_t(stacked(main), imat_t, 0, n_own) + apply_t(stacked(last), imat_t, n_own + n_x, group)
         else:
             both = stacked(jnp.concatenate(outer, axis=1))
-            out_t[place] = out_t[place] + apply_nt(both, imat, n_own, n_x)
+            out_t[place] = out_t[place] + apply_t(both, imat_t, n_own, n_x)
 
     stores = []
 
@@ -547,21 +551,25 @@
                 stores[-1].start()
 
     for step in range(n + 3):
-        for stage, lag in ((leave, 3), (forward, 2), (middle, 1), (adjoint, 0)):
+        for stage, lag in ((adjoint, 0), (middle, 1), (forward, 2), (leave, 3)):
             if 0 <= step - lag < n:
                 stage(step - lag)
+        if step == n:
+            for c in range(n - 2):
+                spare(c)
         if step == n + 1:
             for c in range(n - 2):
                 relay(c)
+            spare(n - 2)
+            spare(n - 1)
+            for c in range(n - 2):
                 finish(0, c)
-        if 0 <= step - 2 < n:
-            spare(step - 2)
     relay(n - 2)
     finish(0, n - 2)
     for c in range(n - 2):
         finish(1, c)
+    finish(0, n - 1)
     relay(n - 1)
-    finish(0, n - 1)
     for c in range(-1, n - 2):
         store(c)
     finish(1, n - 2)
@@ -602,7 +610,8 @@
         *[pltpu.VMEM(item.shape[2:], jnp.int32) for item in (interp_cols, conv_cols, halo_index)],
         f32(rows, feat), f32(*interp_wt.shape[2:]), f32(*conv_wt.shape[2:]), f32(*conv_wt.shape[2:]),
         pltpu.VMEM(conv_cols.shape[2:], jnp.int32), pltpu.VMEM(halo_index.shape[2:], jnp.int32),
-        bf16(2, feat, rows), bf16(2, rows, extent), bf16(2, 2, n_own, extent), bf16(2, n_own, n_slot),
+        bf16(2, feat, rows), bf16(2, rows, extent), bf16(2, extent, rows),
+        bf16(2, 2, n_own, extent), bf16(2, 2, extent, n_own), bf16(2, n_own, n_slot), bf16(2, n_slot, n_own),
         f32(feat, n_own), f32(2, 3, half, group), f32(3, 3, half, group),
         f32(half, n_own), f32(3, half, group), f32(2, half, n_own),
         f32(2, 3, half, group), f32(2, 3, half, group), f32(2, half, group),
@@ -613,7 +622,7 @@
         f32(feat, rows), f32(feat // 128, rows, 128),
     ]
     dma = pltpu.SemaphoreType.DMA
-    scratch += [dma((15 + 4 * len(cuts),)), dma((5 + 14 * len(cuts),)), dma((6,)), dma((feat // 128,))]
+    scratch += [dma((11 + 8 * len(cuts),)), dma((5 + 14 * len(cuts),)), dma((6,)), dma((feat // 128,))]
     return pl.pallas_call(
         functools.partial(pair_kernel, n_ty, cuts),
         out_shape=jax.ShapeDtypeStruct((rows, feat), F32),

time: 83.7 us -> 80.8 us (0.965); the launches traced: 83.5 us -> 79.6 us
  Pallas kernels: 81.8 us -> 77.8 us
    pallas_call x1, Pallas kernels: 81.8 us -> 77.8 us  [pair_call(): pl.pallas_call(functools.partial(pair_kernel, n_ty, cuts), out_shape=jax....]
where the time goes in v4:
time: 80.8 us; the launch traced here: 79.6 us
  Pallas kernels  77.8 us (96%)
  local copies, waits for them, and re-layouts  1.06 us (1%)
    pallas_call x1, Pallas kernels, pair_call(): pl.pallas_call(functools.partial(pair_kernel, n_ty, cuts), out_shape=jax....  77.8 us

profile of v4, /device:TPU:17, one launch (start us, length us, event | category | flops | bytes accessed | tf_op | source)
XLA Modules:
  0.0 79.6 jit_solution(11757696080129638454)
XLA Ops:
  0.7 77.8 %shard_map.73 = f32[512,640]{1,0:T(8,128)S(1)} custom-call(s32[1,1]{1,0:T(1,128)S(6)} %copy.9.valid_ref, f32[512,640]{1,0:T(8,128)} %bitcast.8, f32[4,128,384]{2,1,0:T(8,128)} %bitcast.10, s32[4,384]{1,0:T(4,128)} %bitcast.12, f32[4,128,512]{2,1,0:T(8,128)} %bitcast.9, s32[4,512]{1,0:T(4,128)} %bitcast.11, s32[8,64]{1,0:T(8,128)} %bitcast.13), custom_call_target="tpu_custom_call" | custom-call | tf_op jit(solution)/shard_map/pallas_call | solution.py:626
  78.5 1.1 %copy.10 = f32[1,1,512,640]{3,2,1,0:T(8,128)} copy(f32[1,1,512,640]{3,2,1,0:T(8,128)S(1)} %bitcast.7) | data formatting | bytes 2621440

commit v5 on v4

--- a/solution.py
+++ b/solution.py
@@ -213,7 +213,7 @@
     n_ty, cuts, valid_ref, ctrl_hbm, iwt_hbm, icols_hbm, cwt_hbm, ccols_hbm, halo_hbm,
     out_ref, icols_ref, ccols_ref, halo_ref, ctrl, iwt, cwt, cwt_f, ccols_f, halo_f, xt, imat, imat_t, cmat, cmat_t, pick, pick_t,
     zp, s1, near, zf, r1o, bown, s2, r2, loc2, s3, r3, loc3, vacc,
-    s4o, r4o, r4x, v_r, s6, r6, loc6, s5, r5, out_t, out_v, send_sem, recv_sem, load_sem, store_sem,
+    s4o, r4o, r4x, v_r, s6, r6, loc6, s5, r5, out_t, send_sem, recv_sem, load_sem,
 ):
     rows, feat = ctrl.shape
     half = feat // 2
@@ -251,37 +251,70 @@
         else:
             greet()
 
-    flows, tags = [], {}
+    arrivals, tags = [], {}
+    both_there = jnp.logical_and(there(-1), there(1))
+    one_there = jnp.logical_xor(there(-1), there(1))
 
     class Flow:
-        def __init__(self, src, dst, row_off, flip, tag=None):
-            self.row_off = row_off
-            self.tag = tag or len(flows)
-            key = tags.setdefault(self.tag, [len(tags), None])[0]
-            self.copy = pltpu.make_async_remote_copy(
-                src_ref=src, dst_ref=dst, send_sem=send_sem.at[key], recv_sem=recv_sem.at[len(flows)],
-                device_id=(ty + row_off, far if flip else tx), device_id_type=MESH,
+        def __init__(self, src, dst, tag=None):
+            self.tag = tag or len(arrivals)
+            self.keys = tags.setdefault(self.tag, [len(tags), None])[0], len(arrivals)
+            arrivals.append(self)
+            self.prepare(src, dst)
+
+        def prepare(self, src, dst):
+            self.copy = self.remote(src, dst, ty, far)
+
+        def remote(self, src, dst, to_ty, to_tx):
+            return pltpu.make_async_remote_copy(
+                src_ref=src, dst_ref=dst, send_sem=send_sem.at[self.keys[0]], recv_sem=recv_sem.at[self.keys[1]],
+                device_id=(to_ty, to_tx), device_id_type=MESH,
             )
-            flows.append(self)
-
-        def act(self, sign, action):
-            if self.row_off:
-                pl.when(there(sign * self.row_off))(action)
-            else:
-                action()
 
         def start(self):
             before = tags[self.tag][1]
             if before is not None:
                 before.sent()
             tags[self.tag][1] = self
-            self.act(1, lambda: self.copy.start())
+            self.begin()
+
+        def begin(self):
+            self.copy.start()
 
         def arrived(self):
-            self.act(-1, lambda: self.copy.wait_recv())
+            self.copy.wait_recv()
 
         def sent(self):
-            self.act(1, lambda: self.copy.wait_send())
+            self.copy.wait_send()
+
+    class Pair(Flow):
+        def __init__(self, src, dst, sign, tag=None):
+            self.sign = sign
+            super().__init__(src, dst, tag)
+
+        def prepare(self, src, dst):
+            self.both = self.remote(src, dst, ty, far)
+            self.parts = [
+                self.remote(src.at[k], dst.at[k], ty + step, tx) for k, step in enumerate((self.sign, -self.sign))
+            ]
+
+        def begin(self):
+            for part, step in zip(self.parts, (self.sign, -self.sign)):
+                pl.when(there(step))(part.start)
+
+        def arrived(self):
+            pl.when(both_there)(self.both.wait_recv)
+            pl.when(one_there)(self.parts[0].wait_recv)
+
+        def sent(self):
+            pl.when(both_there)(self.both.wait_send)
+            pl.when(one_there)(self.parts[0].wait_send)
+
+    def settle(keep=()):
+        for entry in tags.values():
+            if entry[1] is not None and entry[1] not in keep:
+                entry[1].sent()
+                entry[1] = None
 
     def go(*items):
         for item in items:
@@ -362,20 +395,20 @@
 
     @pl.when(jnp.logical_not(there(-1)))
     def _():
-        for ref in (near.at[0], r2.at[0], r3.at[1], r4o.at[2], r6.at[1], r5.at[1]):
+        for ref in (near.at[0], r2.at[0], r3.at[1], r4o.at[1], r6.at[1], r5.at[1]):
             blank(ref)
 
     @pl.when(jnp.logical_not(there(1)))
     def _():
-        for ref in (near.at[2], r2.at[1], r3.at[0], r4o.at[0], r6.at[0], r5.at[0]):
+        for ref in (near.at[1], r2.at[1], r3.at[0], r4o.at[0], r6.at[0], r5.at[0]):
             blank(ref)
 
     loads[0].wait()
     pl.semaphore_wait(barrier, 1 + jnp.where(there(-1), 1, 0) + jnp.where(there(1), 1, 0))
     for item in loads[3:]:
         item.wait()
-    tables = go(Flow(ccols_ref, ccols_f, 0, 1), Flow(halo_ref, halo_f, 0, 1))
-    weights = go(Flow(cwt, cwt_f, 0, 1))
+    tables = go(Flow(ccols_ref, ccols_f), Flow(halo_ref, halo_f))
+    weights = go(Flow(cwt, cwt_f))
 
     limit = valid_ref[0, 0]
     loads[1].wait()
@@ -392,17 +425,17 @@
         span = slice(q * half, (q + 1) * half)
         both = jnp.concatenate([xt[0, span], xt[1, span]], axis=0)
         value = apply((xt[0, span], both), imat, n_own, n_slot)
-        s1[0, q], near[1, q], s1[1, q] = (value[:, g * group : (g + 1) * group] for g in range(3))
+        s1[0, q], near[2, q], s1[1, q] = (value[:, g * group : (g + 1) * group] for g in range(3))
         last.append(value[:, n_x:])
     s1[0, 2], s1[1, 2] = packed(jnp.concatenate(last, axis=0))
-    first = go(Flow(s1.at[0], near.at[0], 1, 0), Flow(s1.at[1], near.at[2], -1, 0))
+    first = go(Pair(s1, near.at[0:2], 1))
     for q in range(2):
         span = slice(q * half, (q + 1) * half)
         both = jnp.concatenate([xt[0, span], xt[1, span]], axis=0)
         zp[span] = apply((xt[0, span], both), imat, 0, n_own)
     choose(0, halo_ref, OWN_ORDER)
     wait(first)
-    extra = unpacked(near[0, 2], near[2, 2])
+    extra = unpacked(near[0, 2], near[1, 2])
     for q in range(2):
         span = slice(q * half, (q + 1) * half)
         zp[span] = zp[span] + scatter(0, [extra[span]], n_x)
@@ -410,8 +443,8 @@
     for lo, count in cuts:
         span = pl.ds(lo, count)
         crossed.append(go(
-            Flow(zp.at[theirs(lo, count)], zf.at[span], 0, 1),
-            Flow(near.at[:, far, within(far, lo, count)], r1o.at[:, span], 0, 1),
+            Flow(zp.at[theirs(lo, count)], zf.at[span]),
+            Flow(near.at[:, far, within(far, lo, count)], r1o.at[:, span]),
         ))
     for b in range(blocks):
         dense(cmat.at[0], cmat_t.at[0], b, cwt[b], ccols_ref[b : b + 1, :], OWN_ORDER)
@@ -432,9 +465,7 @@
             sent[1, t, span] = value[t][:, 2 * group : n_x]
             last.append(value[t][:, n_x:])
         sent[0, 2, span], sent[1, 2, span] = blend(last[0], last[1]), blend(last[1], last[0])
-        return go(*[
-            Flow(sent.at[k, :, span], got.at[k, :, span], sign - 2 * k * sign, 0, (tag, k)) for k in range(2)
-        ])
+        return go(Pair(sent.at[:, :, span], got.at[:, :, span], sign, tag))
 
     def swapped(c, got, kept):
         span = pl.ds(*cuts[c])
@@ -452,8 +483,8 @@
         here = within(tx, lo, count)
         wait(crossed[c])
         z = [
-            zp[mine(lo, count)] + scatter(0, [r1o[g, span] for g in range(3)]),
-            zf[span] + scatter(1, [near[g, tx, here] for g in range(3)]),
+            zp[mine(lo, count)] + scatter(0, [r1o[g, span] for g in (0, 2, 1)]),
+            zf[span] + scatter(1, [near[g, tx, here] for g in (0, 2, 1)]),
         ]
         z = [stacked(item) for item in z]
         second[c] = swap(c, s2, r2, loc2, 1, "b", [apply(z[t], cmat.at[t], n_own, n_slot) for t in range(2)])
@@ -479,13 +510,10 @@
             v[t] = vacc[t, span] + apply_t(stacked(slots[t]), cmat_t.at[t], n_own, n_slot)
             vacc[t, span] = v[t]
             if t:
-                whole[c] = go(Flow(vacc.at[1, span], v_r.at[span], 0, 1))
+                whole[c] = go(Flow(vacc.at[1, span], v_r.at[span]))
         value = gather(0, stacked(v[0])[1], 0, n_slot)
-        s4o[0, span], r4o[1, span], s4o[1, span] = (value[:, g * group : (g + 1) * group] for g in range(3))
-        sides[c] = go(
-            Flow(s4o.at[0, span], r4o.at[0, span], -1, 0, ("s", 0)),
-            Flow(s4o.at[1, span], r4o.at[2, span], 1, 0, ("s", 1)),
-        )
+        s4o[0, span], r4o[2, span], s4o[1, span] = (value[:, g * group : (g + 1) * group] for g in range(3))
+        sides[c] = go(Pair(s4o.at[:, span], r4o.at[0:2, span], -1, "s"))
         s6[0, 2, part], s6[1, 2, part] = packed(value[:, n_x:])
         value = gather(1, stacked(v[1])[1], 0, n_x)
         loc6[span] = value[:, group : 2 * group]
@@ -496,33 +524,37 @@
     def leave(c):
         span = pl.ds(*cuts[c])
         wait(sides[c])
-        sixth[c] = go(Flow(r4o.at[:, span], r4x.at[:, span], 0, 1))
-
-    def spare(c):
-        lo, count = cuts[c]
-        part = pl.ds(lo // 2, count // 2)
-        fourth[c] = go(*[
-            Flow(s6.at[k, :, part], r6.at[k, :, part], 2 * k - 1, 0) for k in range(2)
-        ])
-
-    def relay(c):
-        lo, count = cuts[c]
-        part = pl.ds(lo // 2, count // 2)
-        wait(whole[c])
-        s5[0, part], s5[1, part] = packed(gather(0, stacked(v_r[pl.ds(lo, count)])[1], n_x, group))
-        fifth[c] = go(*[Flow(s5.at[k, part], r5.at[k, part], 2 * k - 1, 0) for k in range(2)])
+        sixth[c] = go(Flow(r4o.at[:, span], r4x.at[:, span]))
+
+    def joined(c, count):
+        lo = cuts[c][0]
+        end = sum(cuts[c + count - 1])
+        return pl.ds(lo // 2, (end - lo) // 2)
+
+    def spare(c, count):
+        part = joined(c, count)
+        fourth[c] = go(Pair(s6.at[:, :, part], r6.at[:, :, part], -1))
+
+    def relay(c, count=1):
+        for k in range(c, c + count):
+            wait(whole[k])
+            lo, width = cuts[k]
+            part = pl.ds(lo // 2, width // 2)
+            s5[0, part], s5[1, part] = packed(gather(0, stacked(v_r[pl.ds(lo, width)])[1], n_x, group))
+        part = joined(c, count)
+        fifth[c] = go(Pair(s5.at[:, part], r5.at[:, part], -1))
 
     def finish(q, c, stages=(0, 1)):
         lo, count = cuts[c]
         span, part = pl.ds(lo, count), pl.ds(lo // 2, count // 2)
         place = theirs(lo, count) if q else mine(lo, count)
         if 0 in stages:
-            wait(fifth[c] if q else fourth[c])
+            wait(fifth.get(c, ()) if q else fourth.get(c, ()))
             last = unpacked(r5[0, part], r5[1, part]) if q else unpacked(r6[0, 2, part], r6[1, 2, part])
             main = v_r[span] if q else vacc[0, span]
         if 1 in stages and q:
             wait(sixth[c])
-            outer = [r4x[g, span] for g in range(3)]
+            outer = [r4x[g, span] for g in (0, 2, 1)]
         elif 1 in stages:
             outer = [jnp.concatenate([r6[k, 0, part], r6[k, 1, part]], axis=0) for k in range(2)]
             outer.insert(1, loc6[span])
@@ -535,8 +567,6 @@
             both = stacked(jnp.concatenate(outer, axis=1))
             out_t[place] = out_t[place] + apply_t(both, imat_t, n_own, n_x)
 
-    stores = []
-
     def ready(r):
         return max([c for c in range(n) if half + cuts[c][0] < (r + 1) * tile], default=-1)
 
@@ -546,41 +576,37 @@
                 block = far * r + tx * (feat // tile - 1 - r)
                 span = pl.ds(pl.multiple_of(block * tile, tile), tile)
                 live = lax.broadcasted_iota(jnp.int32, (rows, tile), 0) < limit
-                out_v[r] = jnp.where(live, out_t[span].T, 0.0)
-                stores.append(pltpu.make_async_copy(out_v.at[r], out_ref.at[:, span], store_sem.at[r]))
-                stores[-1].start()
+                out_ref[:, span] = jnp.where(live, out_t[span].T, 0.0)
 
     for step in range(n + 3):
-        for stage, lag in ((adjoint, 0), (middle, 1), (forward, 2), (leave, 3)):
+        order = ((adjoint, 0), (middle, 1), (leave, 3), (forward, 2))
+        if step > n:
+            order = ((forward, 2), (leave, 3))
+        for stage, lag in order:
             if 0 <= step - lag < n:
                 stage(step - lag)
         if step == n:
-            for c in range(n - 2):
-                spare(c)
+            spare(0, n - 2)
         if step == n + 1:
-            for c in range(n - 2):
-                relay(c)
-            spare(n - 2)
-            spare(n - 1)
+            relay(0, n - 2)
+            spare(n - 2, 2)
             for c in range(n - 2):
                 finish(0, c)
     relay(n - 2)
     finish(0, n - 2)
+    relay(n - 1)
     for c in range(n - 2):
         finish(1, c)
     finish(0, n - 1)
-    relay(n - 1)
     for c in range(-1, n - 2):
         store(c)
     finish(1, n - 2)
     store(n - 2)
+    settle(sixth[n - 1] + fifth[n - 1])
     finish(1, n - 1, (0,))
     finish(1, n - 1, (1,))
     store(n - 1)
-    for _, item in tags.values():
-        item.sent()
-    for item in stores:
-        item.wait()
+    settle()
 
 
 def split(total, parts):
@@ -619,15 +645,15 @@
         f32(2, half, group), f32(3, half, group), f32(3, half, group), f32(half, n_own),
         f32(2, 3, half // 2, group), f32(2, 3, half // 2, group), f32(half, group),
         f32(2, half // 2, group), f32(2, half // 2, group),
-        f32(feat, rows), f32(feat // 128, rows, 128),
+        f32(feat, rows),
     ]
     dma = pltpu.SemaphoreType.DMA
-    scratch += [dma((11 + 8 * len(cuts),)), dma((5 + 14 * len(cuts),)), dma((6,)), dma((feat // 128,))]
+    scratch += [dma((8 + 5 * len(cuts) + 1,)), dma((5 + 8 * len(cuts),)), dma((6,))]
     return pl.pallas_call(
         functools.partial(pair_kernel, n_ty, cuts),
         out_shape=jax.ShapeDtypeStruct((rows, feat), F32),
         in_specs=[pl.BlockSpec(memory_space=pltpu.SMEM)] + [hbm] * 6,
-        out_specs=pl.BlockSpec(memory_space=pl.ANY),
+        out_specs=vmem,
         scratch_shapes=scratch,
         compiler_params=pltpu.CompilerParams(
             collective_id=0, has_side_effects=True, vmem_limit_bytes=52 * 1024 * 1024

time: 80.8 us -> 80.3 us (level)
  no operation moved by 1% of the time
where the time goes in v5:
time: 80.3 us; the launch traced here: 79.2 us
  Pallas kernels  77.5 us (97%)
  local copies, waits for them, and re-layouts  1.06 us (1%)
    pallas_call x1, Pallas kernels, pair_call(): pl.pallas_call(functools.partial(pair_kernel, n_ty, cuts), out_shape=jax....  77.5 us

profile of v5, /device:TPU:17, one launch (start us, length us, event | category | flops | bytes accessed | tf_op | source)
XLA Modules:
  0.0 79.2 jit_solution(4169511287355655712)
XLA Ops:
  0.7 77.5 %shard_map.73 = f32[512,640]{1,0:T(8,128)S(1)} custom-call(s32[1,1]{1,0:T(1,128)S(6)} %copy.9.valid_ref, f32[512,640]{1,0:T(8,128)} %bitcast.8, f32[4,128,384]{2,1,0:T(8,128)} %bitcast.10, s32[4,384]{1,0:T(4,128)} %bitcast.12, f32[4,128,512]{2,1,0:T(8,128)} %bitcast.9, s32[4,512]{1,0:T(4,128)} %bitcast.11, s32[8,64]{1,0:T(8,128)} %bitcast.13), custom_call_target="tpu_custom_call" | custom-call | tf_op jit(solution)/shard_map/pallas_call | solution.py:652
  78.2 1.1 %copy.10 = f32[1,1,512,640]{3,2,1,0:T(8,128)} copy(f32[1,1,512,640]{3,2,1,0:T(8,128)S(1)} %bitcast.7) | data formatting | bytes 2621440

commit v6 on v5

--- a/solution.py
+++ b/solution.py
@@ -407,8 +407,8 @@
     pl.semaphore_wait(barrier, 1 + jnp.where(there(-1), 1, 0) + jnp.where(there(1), 1, 0))
     for item in loads[3:]:
         item.wait()
-    tables = go(Flow(ccols_ref, ccols_f), Flow(halo_ref, halo_f))
-    weights = go(Flow(cwt, cwt_f))
+    tables = go(Flow(ccols_ref, ccols_f, "t0"), Flow(halo_ref, halo_f, "t1"))
+    weights = go(Flow(cwt, cwt_f, "x"))
 
     limit = valid_ref[0, 0]
     loads[1].wait()
@@ -428,7 +428,7 @@
         s1[0, q], near[2, q], s1[1, q] = (value[:, g * group : (g + 1) * group] for g in range(3))
         last.append(value[:, n_x:])
     s1[0, 2], s1[1, 2] = packed(jnp.concatenate(last, axis=0))
-    first = go(Pair(s1, near.at[0:2], 1))
+    first = go(Pair(s1, near.at[0:2], 1, "f"))
     for q in range(2):
         span = slice(q * half, (q + 1) * half)
         both = jnp.concatenate([xt[0, span], xt[1, span]], axis=0)
@@ -440,11 +440,11 @@
         span = slice(q * half, (q + 1) * half)
         zp[span] = zp[span] + scatter(0, [extra[span]], n_x)
     crossed = []
-    for lo, count in cuts:
+    for c, (lo, count) in enumerate(cuts):
         span = pl.ds(lo, count)
         crossed.append(go(
-            Flow(zp.at[theirs(lo, count)], zf.at[span]),
-            Flow(near.at[:, far, within(far, lo, count)], r1o.at[:, span]),
+            Flow(zp.at[theirs(lo, count)], zf.at[span], ("z", c)),
+            Flow(near.at[:, far, within(far, lo, count)], r1o.at[:, span], ("g", c)),
         ))
     for b in range(blocks):
         dense(cmat.at[0], cmat_t.at[0], b, cwt[b], ccols_ref[b : b + 1, :], OWN_ORDER)
@@ -510,7 +510,7 @@
             v[t] = vacc[t, span] + apply_t(stacked(slots[t]), cmat_t.at[t], n_own, n_slot)
             vacc[t, span] = v[t]
             if t:
-                whole[c] = go(Flow(vacc.at[1, span], v_r.at[span]))
+                whole[c] = go(Flow(vacc.at[1, span], v_r.at[span], ("z", c)))
         value = gather(0, stacked(v[0])[1], 0, n_slot)
         s4o[0, span], r4o[2, span], s4o[1, span] = (value[:, g * group : (g + 1) * group] for g in range(3))
         sides[c] = go(Pair(s4o.at[:, span], r4o.at[0:2, span], -1, "s"))
@@ -524,7 +524,7 @@
     def leave(c):
         span = pl.ds(*cuts[c])
         wait(sides[c])
-        sixth[c] = go(Flow(r4o.at[:, span], r4x.at[:, span]))
+        sixth[c] = go(Flow(r4o.at[:, span], r4x.at[:, span], ("g", c)))
 
     def joined(c, count):
         lo = cuts[c][0]
@@ -533,7 +533,7 @@
 
     def spare(c, count):
         part = joined(c, count)
-        fourth[c] = go(Pair(s6.at[:, :, part], r6.at[:, :, part], -1))
+        fourth[c] = go(Pair(s6.at[:, :, part], r6.at[:, :, part], -1, "b" if c else "f"))
 
     def relay(c, count=1):
         for k in range(c, c + count):
@@ -542,7 +542,7 @@
             part = pl.ds(lo // 2, width // 2)
             s5[0, part], s5[1, part] = packed(gather(0, stacked(v_r[pl.ds(lo, width)])[1], n_x, group))
         part = joined(c, count)
-        fifth[c] = go(Pair(s5.at[:, part], r5.at[:, part], -1))
+        fifth[c] = go(Pair(s5.at[:, part], r5.at[:, part], -1, ("t0", "t1", "x")[len(fifth)]))
 
     def finish(q, c, stages=(0, 1)):
         lo, count = cuts[c]
@@ -648,7 +648,7 @@
         f32(feat, rows),
     ]
     dma = pltpu.SemaphoreType.DMA
-    scratch += [dma((8 + 5 * len(cuts) + 1,)), dma((5 + 8 * len(cuts),)), dma((6,))]
+    scratch += [dma((7 + 2 * len(cuts),)), dma((5 + 8 * len(cuts),)), dma((6,))]
     return pl.pallas_call(
         functools.partial(pair_kernel, n_ty, cuts),
         out_shape=jax.ShapeDtypeStruct((rows, feat), F32),

time: 80.3 us -> 80.2 us (level)
  no operation moved by 1% of the time
where the time goes in v6:
time: 80.2 us; the launch traced here: 79.1 us
  Pallas kernels  77.4 us (97%)
  local copies, waits for them, and re-layouts  1.06 us (1%)
    pallas_call x1, Pallas kernels, pair_call(): pl.pallas_call(functools.partial(pair_kernel, n_ty, cuts), out_shape=jax....  77.4 us

profile of v6, /device:TPU:17, one launch (start us, length us, event | category | flops | bytes accessed | tf_op | source)
XLA Modules:
  0.0 79.1 jit_solution(17494119179253243328)
XLA Ops:
  0.7 77.4 %shard_map.73 = f32[512,640]{1,0:T(8,128)S(1)} custom-call(s32[1,1]{1,0:T(1,128)S(6)} %copy.9.valid_ref, f32[512,640]{1,0:T(8,128)} %bitcast.8, f32[4,128,384]{2,1,0:T(8,128)} %bitcast.10, s32[4,384]{1,0:T(4,128)} %bitcast.12, f32[4,128,512]{2,1,0:T(8,128)} %bitcast.9, s32[4,512]{1,0:T(4,128)} %bitcast.11, s32[8,64]{1,0:T(8,128)} %bitcast.13), custom_call_target="tpu_custom_call" | custom-call | tf_op jit(solution)/shard_map/pallas_call | solution.py:652
  78.0 1.1 %copy.10 = f32[1,1,512,640]{3,2,1,0:T(8,128)} copy(f32[1,1,512,640]{3,2,1,0:T(8,128)S(1)} %bitcast.7) | data formatting | bytes 2621440
